TPU v7x, 32 devices: a whole 2x2x4 slice. The times are simulated.
32 devices in a mesh: row: 4 (over z), col: 8 (over y, x, core).
Axes of the slice: x: 2, y: 2, z: 4, core: 2. Of those that a mesh axis runs over, the one named last changes fastest.
Arguments:
- prior: float32 [80, 30, 16384], P(None, None, ('row', 'col')), may hold values from -6 to 6
- ocean_mask: int32 [16384], P(('row', 'col')), may hold values from 0 to 1
- tile_order: int32 [32], replicated, may hold values from 0 to 31, each once
- obs_cell: int32 [4, 128], replicated, may hold values from 0 to 16383
- obs_stack: int32 [4, 128], replicated, may hold values from 0 to 29
- obs_values: float32 [4, 128], replicated, may hold values from -8 to 8
- window_start: int32 [4, 128], replicated, may hold values from 0 to 16383
- window_span: int32 [4, 128], replicated, may hold values from 1024 to 4096
- gain_mean: float32 [4, 128, 128], replicated, may hold values from -0.2 to 0.8
- gain_spread: float32 [4, 128, 128], replicated, may hold values from -0.2 to 0.4
Outputs:
- posterior: float32 [80, 30, 16384], P(None, None, ('row', 'col'))
Inputs may be any that keep to these rules, and one draw needn't show every extreme that they name: `tile_order`: each curve tile appears once.
All inputs are finite; a program needn't handle non-finite values.
Results may differ from a plain program's by a relative error of at most 0.0001.
Values sent between devices are 32-bit elements; how exact they have to be, the bound alone decides.
A program may use at most 64 MiB of HBM per device.

v0:
```python
import functools

import jax
import jax.numpy as jnp
from jax import lax
from jax.experimental import pallas as pl
from jax.experimental.pallas import tpu as pltpu
from jax.sharding import PartitionSpec as P

MESH = pl.DeviceIdType.MESH
NT = (((1,), (1,)), ((), ()))
SLOTS = 64
SIZES = (48, 80)


def device_number():
    return lax.axis_index("row") * lax.axis_size("col") + lax.axis_index("col")


def round_up(number, step):
    return (number + step - 1) // step * step


def extract_kernel(
    columns, rows, order_s, cell_s, stack_s, ocean_s, x_hbm, out_ref, found, buf, acc, sems
):
    batches, obs = cell_s.shape
    members = buf.shape[1]
    chunks, chunk_rows, _ = out_ref.shape
    base = order_s[device_number()] * columns
    acc[...] = jnp.zeros_like(acc)

    count = 0
    for batch in range(batches):

        def scan(j, count, batch=batch):
            found[count] = batch * obs + j
            local = cell_s[batch, j] - base
            here = jnp.logical_and(local >= 0, local < columns)
            return count + here.astype(jnp.int32)

        count = lax.fori_loop(0, obs, scan, count, unroll=32)
    lane = lax.broadcasted_iota(jnp.int32, (members, obs), 1)
    row = lax.broadcasted_iota(jnp.int32, (8, obs), 0)
    lane8 = lax.broadcasted_iota(jnp.int32, (8, obs), 1)

    def fetch(index, slot):
        b, j = index // obs, index % obs
        local = cell_s[b, j] - base
        tile = pl.multiple_of(local // 128 * 128, 128)
        return pltpu.make_async_copy(
            x_hbm.at[stack_s[b, j], :, pl.ds(tile, 128)], buf.at[slot], sems.at[slot]
        )

    def group(number, carry):
        first = number * SLOTS
        held = jnp.minimum(count - first, SLOTS)

        def start(slot, c):
            fetch(found[first + slot], slot).start()
            return c

        def finish(slot, c):
            index = found[first + slot]
            fetch(index, slot).wait()
            b, j = index // obs, index % obs
            local = cell_s[b, j] - base
            moved = pltpu.roll(buf[slot], (j - local % 128 + 128) % 128, axis=1)
            top = pl.multiple_of(b * rows, 8)
            acc[pl.ds(top, members), :] = jnp.where(
                lane == j, moved, acc[pl.ds(top, members), :]
            )
            flag = jnp.where(row == 0, ocean_s[local].astype(jnp.float32), 0.0)
            low = pl.multiple_of(top + members, 8)
            acc[pl.ds(low, 8), :] = jnp.where(lane8 == j, flag, acc[pl.ds(low, 8), :])
            return c

        lax.fori_loop(0, held, start, 0)
        lax.fori_loop(0, held, finish, 0)
        return carry

    lax.fori_loop(0, (count + SLOTS - 1) // SLOTS, group, 0)
    for chunk in range(chunks):
        out_ref[chunk] = acc[chunk * chunk_rows : (chunk + 1) * chunk_rows, :]


def exchange_kernel(part, out, landed, send_a, recv_a, send_b, recv_b):
    devices = part.shape[0]
    cols = lax.axis_size("col")
    me = device_number()

    def peer(step):
        return lax.rem(me + step, devices)

    def place(number):
        return (number // cols, lax.rem(number, cols))

    barrier = pltpu.get_barrier_semaphore()

    def greet(step, c):
        pl.semaphore_signal(barrier, inc=1, device_id=place(peer(step)), device_id_type=MESH)
        return c

    lax.fori_loop(1, devices, greet, 0)
    pl.semaphore_wait(barrier, devices - 1)

    def scatter(other, slot):
        return pltpu.make_async_remote_copy(
            src_ref=part.at[other],
            dst_ref=landed.at[slot],
            send_sem=send_a.at[other],
            recv_sem=recv_a.at[slot],
            device_id=place(other),
            device_id_type=MESH,
        )

    def gather(other, slot):
        return pltpu.make_async_remote_copy(
            src_ref=out.at[me],
            dst_ref=out.at[slot],
            send_sem=send_b.at[other],
            recv_sem=recv_b.at[slot],
            device_id=place(other),
            device_id_type=MESH,
        )

    def each(act):
        def step(number, c):
            act(peer(number))
            return c

        lax.fori_loop(1, devices, step, 0)

    each(lambda other: scatter(other, me).start())
    landed[me] = part[me]
    each(lambda other: scatter(other, other).wait_recv())
    out[me] = jnp.sum(landed[...], axis=0)
    each(lambda other: gather(other, me).start())
    each(lambda other: gather(other, other).wait_recv())
    each(lambda other: scatter(other, me).wait_send())
    each(lambda other: gather(other, me).wait_send())


def split(values):
    high = values.astype(jnp.bfloat16)
    low = (values - high.astype(jnp.float32)).astype(jnp.bfloat16)
    return high, low


def triple(values, axis):
    high, low = split(values)
    return jnp.concatenate([high, low, high], axis=axis)


def product(left, right):
    high, low = split(left)
    return lax.dot_general(
        jnp.concatenate([high, high, low], axis=1),
        triple(right, 1),
        NT,
        preferred_element_type=jnp.float32,
    )


def update_kernel(
    rows,
    order_s,
    ocean_ref,
    cell_ref,
    start_ref,
    span_ref,
    value_ref,
    mean_ref,
    spread_ref,
    shared_ref,
    x_hbm,
    y_hbm,
    xt,
    flat,
    side_a,
    side_d,
    lhs_a,
    lhs_d,
    weight,
    sem_in,
    sem_out,
):
    stack, members, columns = xt.shape
    batches, obs = cell_ref.shape
    chunks, chunk_rows, _ = shared_ref.shape

    def incoming(v):
        return pltpu.make_async_copy(x_hbm.at[v], xt.at[v], sem_in.at[v])

    def outgoing(v):
        return pltpu.make_async_copy(xt.at[v], y_hbm.at[v], sem_out.at[v])

    def begin(v, c):
        incoming(v).start()
        return c

    lax.fori_loop(0, stack, begin, 0)

    for chunk in range(chunks):
        flat[chunk * chunk_rows : (chunk + 1) * chunk_rows, :] = shared_ref[chunk]
    base = (order_s[device_number()] * columns).astype(jnp.float32)
    places = base + lax.broadcasted_iota(jnp.int32, (1, columns), 1).astype(jnp.float32)
    ocean = ocean_ref[...].astype(jnp.float32)
    cells = cell_ref[...].astype(jnp.float32)
    starts = start_ref[...].astype(jnp.float32)
    ends = (start_ref[...] + span_ref[...]).astype(jnp.float32)
    priors = [flat[b * rows : b * rows + members, :] for b in range(batches)]
    flags = [flat[b * rows + members : b * rows + members + 1, :] for b in range(batches)]
    scale = 1.0 / (members - 1.0)
    meets = jnp.logical_and(starts < base + columns, ends > base).astype(jnp.float32)
    before = lax.broadcasted_iota(jnp.int32, (obs, obs), 0) < lax.broadcasted_iota(
        jnp.int32, (obs, obs), 1
    )
    ranks = jnp.dot(
        jnp.concatenate([meets, jnp.zeros((16 - batches, obs), jnp.float32)], axis=0).astype(
            jnp.bfloat16
        ),
        before.astype(jnp.bfloat16),
        preferred_element_type=jnp.float32,
    )
    most = jnp.max(jnp.sum(meets, axis=1)).astype(jnp.int32)

    for b in range(batches):
        now = priors[b]
        centre = jnp.mean(now, axis=0, keepdims=True)
        anomalies = now - centre
        innovation = jnp.broadcast_to(value_ref[b : b + 1, :] - centre, (16, obs))
        mean_weights = product(innovation, mean_ref[b])[0:1]
        delta = mean_weights - product(anomalies, spread_ref[b])
        scaled = anomalies * scale
        high = scaled.astype(jnp.bfloat16).astype(jnp.float32)
        stacked = jnp.concatenate([high, high, scaled - high], axis=0)
        side_a[b] = stacked.astype(jnp.bfloat16)
        d_high, d_low = split(delta)
        side_d[b, 0] = d_high
        side_d[b, 1] = d_low
        if b + 1 < batches:
            start_of = jnp.transpose(jnp.broadcast_to(starts[b : b + 1], (128, obs)))[:, 0:1]
            end_of = jnp.transpose(jnp.broadcast_to(ends[b : b + 1], (128, obs)))[:, 0:1]
            later = jnp.concatenate(priors[b + 1 :], axis=1)
            cell_row = jnp.concatenate([cells[a : a + 1] for a in range(b + 1, batches)], axis=1)
            flag_row = jnp.concatenate(flags[b + 1 :], axis=1)
            inside = jnp.where(
                jnp.logical_and(cell_row >= start_of, cell_row < end_of), flag_row, 0.0
            )
            gain = inside * jnp.dot(
                jnp.transpose(stacked).astype(jnp.bfloat16),
                triple(later, 0),
                preferred_element_type=jnp.float32,
            )
            later = later + jnp.dot(
                jnp.concatenate([d_high, d_high, d_low], axis=1),
                triple(gain, 0),
                preferred_element_type=jnp.float32,
            )
            for a in range(b + 1, batches):
                priors[a] = later[:, (a - b - 1) * obs : (a - b) * obs]

    together = 2 if stack % 2 == 0 else 1

    def sweep_with(kept):
        slot = lax.broadcasted_iota(jnp.int32, (kept, obs), 0).astype(jnp.float32)
        for b in range(batches):
            chosen = jnp.logical_and(slot == ranks[b : b + 1], meets[b : b + 1] > 0.0)
            start_of = jnp.sum(jnp.where(chosen, starts[b : b + 1], 0.0), axis=1, keepdims=True)
            end_of = jnp.sum(jnp.where(chosen, ends[b : b + 1], 0.0), axis=1, keepdims=True)
            weight[b, 0:kept] = jnp.where(
                jnp.logical_and(places >= start_of, places < end_of), ocean, 0.0
            )
            pick = chosen.astype(jnp.bfloat16)
            none = jnp.zeros_like(pick)
            lhs_a[b, 0:kept] = lax.dot_general(
                pick, side_a[b], NT, preferred_element_type=jnp.float32
            ).astype(jnp.bfloat16)
            lhs_d[b, :, 0 : 3 * kept] = (
                lax.dot_general(
                    side_d[b, 0],
                    jnp.concatenate([pick, pick, none], axis=0),
                    NT,
                    preferred_element_type=jnp.float32,
                )
                + lax.dot_general(
                    side_d[b, 1],
                    jnp.concatenate([none, none, pick], axis=0),
                    NT,
                    preferred_element_type=jnp.float32,
                )
            ).astype(jnp.bfloat16)

        def sweep(number, c):
            levels = [number * together + k for k in range(together)]
            for v in levels:
                incoming(v).wait()
            values = [xt[v] for v in levels]
            for b in range(batches):
                gains = []
                for k in range(together):
                    gain = weight[b, 0:kept] * jnp.dot(
                        lhs_a[b, 0:kept],
                        triple(values[k], 0),
                        preferred_element_type=jnp.float32,
                    )
                    gains.append(triple(gain, 0))
                for k in range(together):
                    values[k] = values[k] + jnp.dot(
                        lhs_d[b, :, 0 : 3 * kept], gains[k], preferred_element_type=jnp.float32
                    )
            for k in range(together):
                xt[levels[k]] = values[k]
            for v in levels:
                outgoing(v).start()
            return c

        lax.fori_loop(0, stack // together, sweep, 0)

    sizes = [kept for kept in SIZES if kept < obs] + [obs]
    for low, kept in zip([-1] + sizes[:-1], sizes):
        pl.when(jnp.logical_and(most > low, most <= kept))(functools.partial(sweep_with, kept))

    def end(v, c):
        outgoing(v).wait()
        return c

    lax.fori_loop(0, stack, end, 0)


def per_device(
    prior,
    ocean_mask,
    tile_order,
    obs_cell,
    obs_stack,
    obs_values,
    window_start,
    window_span,
    gain_mean,
    gain_spread,
):
    members, stack, columns = prior.shape
    batches, obs = obs_cell.shape
    devices = tile_order.shape[0]
    rows = members + 8
    chunk_rows = -(-batches * rows // devices)
    smem = pl.BlockSpec(memory_space=pltpu.SMEM)
    vmem = pl.BlockSpec(memory_space=pltpu.VMEM)
    hbm = pl.BlockSpec(memory_space=pl.ANY)
    shared_shape = jax.ShapeDtypeStruct((devices, chunk_rows, obs), jnp.float32)
    flat_rows = round_up(devices * chunk_rows, 8)

    levels = jnp.transpose(prior, (1, 0, 2))
    part = pl.pallas_call(
        functools.partial(extract_kernel, columns, rows),
        out_shape=shared_shape,
        in_specs=[smem, smem, smem, smem, hbm],
        out_specs=vmem,
        scratch_shapes=[
            pltpu.SMEM((batches * obs + 1,), jnp.int32),
            pltpu.VMEM((SLOTS, members, 128), jnp.float32),
            pltpu.VMEM((flat_rows, obs), jnp.float32),
            pltpu.SemaphoreType.DMA((SLOTS,)),
        ],
        name="extract",
    )(tile_order, obs_cell, obs_stack, ocean_mask, levels)

    shared = pl.pallas_call(
        exchange_kernel,
        out_shape=shared_shape,
        in_specs=[vmem],
        out_specs=vmem,
        scratch_shapes=[pltpu.VMEM((devices, chunk_rows, obs), jnp.float32)]
        + [pltpu.SemaphoreType.DMA((devices,))] * 4,
        compiler_params=pltpu.CompilerParams(collective_id=0, has_side_effects=True),
        name="exchange",
    )(part)

    updated = pl.pallas_call(
        functools.partial(update_kernel, rows),
        out_shape=jax.ShapeDtypeStruct(levels.shape, levels.dtype),
        in_specs=[smem] + [vmem] * 8 + [hbm],
        out_specs=hbm,
        scratch_shapes=[
            pltpu.VMEM((stack, members, columns), jnp.float32),
            pltpu.VMEM((flat_rows, obs), jnp.float32),
            pltpu.VMEM((batches, 3 * members, obs), jnp.bfloat16),
            pltpu.VMEM((batches, 2, members, obs), jnp.bfloat16),
            pltpu.VMEM((batches, obs, 3 * members), jnp.bfloat16),
            pltpu.VMEM((batches, members, 3 * obs), jnp.bfloat16),
            pltpu.VMEM((batches, obs, columns), jnp.float32),
            pltpu.SemaphoreType.DMA((stack,)),
            pltpu.SemaphoreType.DMA((stack,)),
        ],
        name="update",
    )(
        tile_order,
        ocean_mask.reshape(1, columns),
        obs_cell,
        window_start,
        window_span,
        obs_values,
        gain_mean,
        gain_spread,
        shared,
        levels,
    )
    return jnp.transpose(updated, (1, 0, 2))


def solution(mesh):
    in_specs = (P(None, None, ("row", "col")), P(("row", "col"))) + (P(),) * 8
    return jax.shard_map(
        per_device,
        mesh=mesh,
        in_specs=in_specs,
        out_specs=P(None, None, ("row", "col")),
        check_vma=False,
    )
```

profile of v0, /device:TPU:1, one launch (start us, length us, event | category | flops | bytes accessed | tf_op | source)
XLA Modules:
  0.0 53.0 jit_solution(5123062299725723047)
XLA Ops:
  0.0 5.7 %extract.1.part = f32[32,11,128]{2,1,0:T(8,128)} custom-call(s32[32]{0:T(128)} %order_s.3, s32[4,128]{1,0:T(4,128)} %cell_ref.1, s32[4,128]{1,0:T(4,128)} %stack_s.1, s32[512]{0:T(512)} %ocean_s.1, f32[30,80,512]{2,1,0:T(8,128)} %bitcast.3), custom_call_target="tpu_custom_call" | custom-call | tf_op jit(solution)/shard_map/extract/pallas_call | solution.py:356
  5.7 22.6 %exchange.1.shared_ref = f32[32,11,128]{2,1,0:T(8,128)} custom-call(f32[32,11,128]{2,1,0:T(8,128)} %extract.1.part), custom_call_target="tpu_custom_call" | custom-call | tf_op jit(solution)/shard_map/exchange/pallas_call | solution.py:370
  28.4 24.6 %update.1 = f32[30,80,512]{2,1,0:T(8,128)} custom-call(s32[32]{0:T(128)} %order_s.3, s32[1,512]{1,0:T(1,128)} %bitcast.5, s32[4,128]{1,0:T(4,128)} %cell_ref.1, s32[4,128]{1,0:T(4,128)} %start_ref.1, s32[4,128]{1,0:T(4,128)} %span_ref.1, f32[4,128]{1,0:T(4,128)} %value_ref.1, f32[4,128,128]{2,1,0:T(8,128)} %mean_ref.1, f32[4,128,128]{2,1,0:T(8,128)} %spread_ref.1, ...), custom_call_target="tpu_custom_call" | custom-call | tf_op jit(solution)/shard_map/update/pallas_call | solution.py:381
where the time goes:
time: 53.4 us; the launch traced here: 53 us
  Pallas kernels  53 us (99%)
    pallas_call x1, Pallas kernels, per_device(): pl.pallas_call(functools.partial(update_kernel, rows), out_shape=jax.Shap...  24.6 us
    pallas_call x1, Pallas kernels, per_device(): pl.pallas_call(exchange_kernel, out_shape=shared_shape, in_specs=[vmem],...  22.6 us
    pallas_call x1, Pallas kernels, per_device(): pl.pallas_call(functools.partial(extract_kernel, columns, rows), out_shap...  5.71 us

commit v1 on v0

--- a/solution.py
+++ b/solution.py
@@ -261,7 +261,7 @@
             for a in range(b + 1, batches):
                 priors[a] = later[:, (a - b - 1) * obs : (a - b) * obs]
 
-    together = 2 if stack % 2 == 0 else 1
+    together = max(k for k in range(1, 7) if stack % k == 0)
 
     def sweep_with(kept):
         slot = lax.broadcasted_iota(jnp.int32, (kept, obs), 0).astype(jnp.float32)

time: 53.4 us -> 42.5 us (0.80)
  Pallas kernels: 53 us -> 41.8 us
    pallas_call x1, Pallas kernels: 24.6 us -> 14.2 us  [per_device(): pl.pallas_call(functools.partial(update_kernel, rows), out_shape=jax.Shap...]
    pallas_call x1, Pallas kernels: 22.6 us -> 21.2 us  [per_device(): pl.pallas_call(exchange_kernel, out_shape=shared_shape, in_specs=[vmem],...]
    pallas_call x1, Pallas kernels: 5.71 us -> 6.4 us  [per_device(): pl.pallas_call(functools.partial(extract_kernel, columns, rows), out_shap...]
where the time goes in v1:
time: 42.5 us; the launch traced here: 41.8 us
  Pallas kernels  41.8 us (98%)
    pallas_call x1, Pallas kernels, per_device(): pl.pallas_call(exchange_kernel, out_shape=shared_shape, in_specs=[vmem],...  21.2 us
    pallas_call x1, Pallas kernels, per_device(): pl.pallas_call(functools.partial(update_kernel, rows), out_shape=jax.Shap...  14.2 us
    pallas_call x1, Pallas kernels, per_device(): pl.pallas_call(functools.partial(extract_kernel, columns, rows), out_shap...  6.4 us

profile of v1, /device:TPU:1, one launch (start us, length us, event | category | flops | bytes accessed | tf_op | source)
XLA Modules:
  0.0 41.8 jit_solution(17534161167801004425)
XLA Ops:
  0.0 6.4 %extract.1.part = f32[32,11,128]{2,1,0:T(8,128)} custom-call(s32[32]{0:T(128)} %order_s.3, s32[4,128]{1,0:T(4,128)} %cell_ref.1, s32[4,128]{1,0:T(4,128)} %stack_s.1, s32[512]{0:T(512)} %ocean_s.1, f32[30,80,512]{2,1,0:T(8,128)} %bitcast.3), custom_call_target="tpu_custom_call" | custom-call | tf_op jit(solution)/shard_map/extract/pallas_call | solution.py:356
  6.4 21.2 %exchange.1.shared_ref = f32[32,11,128]{2,1,0:T(8,128)} custom-call(f32[32,11,128]{2,1,0:T(8,128)} %extract.1.part), custom_call_target="tpu_custom_call" | custom-call | tf_op jit(solution)/shard_map/exchange/pallas_call | solution.py:370
  27.6 14.2 %update.1 = f32[30,80,512]{2,1,0:T(8,128)} custom-call(s32[32]{0:T(128)} %order_s.3, s32[1,512]{1,0:T(1,128)} %bitcast.5, s32[4,128]{1,0:T(4,128)} %cell_ref.1, s32[4,128]{1,0:T(4,128)} %start_ref.1, s32[4,128]{1,0:T(4,128)} %span_ref.1, f32[4,128]{1,0:T(4,128)} %value_ref.1, f32[4,128,128]{2,1,0:T(8,128)} %mean_ref.1, f32[4,128,128]{2,1,0:T(8,128)} %spread_ref.1, ...), custom_call_target="tpu_custom_call" | custom-call | tf_op jit(solution)/shard_map/update/pallas_call | solution.py:381

commit v2 on v1

--- a/solution.py
+++ b/solution.py
@@ -1,4 +1,5 @@
 import functools
+import math
 
 import jax
 import jax.numpy as jnp
@@ -9,7 +10,6 @@
 
 MESH = pl.DeviceIdType.MESH
 NT = (((1,), (1,)), ((), ()))
-SLOTS = 64
 SIZES = (48, 80)
 
 
@@ -21,124 +21,241 @@
     return (number + step - 1) // step * step
 
 
-def extract_kernel(
-    columns, rows, order_s, cell_s, stack_s, ocean_s, x_hbm, out_ref, found, buf, acc, sems
-):
-    batches, obs = cell_s.shape
-    members = buf.shape[1]
-    chunks, chunk_rows, _ = out_ref.shape
-    base = order_s[device_number()] * columns
-    acc[...] = jnp.zeros_like(acc)
-
-    count = 0
-    for batch in range(batches):
-
-        def scan(j, count, batch=batch):
-            found[count] = batch * obs + j
-            local = cell_s[batch, j] - base
-            here = jnp.logical_and(local >= 0, local < columns)
-            return count + here.astype(jnp.int32)
-
-        count = lax.fori_loop(0, obs, scan, count, unroll=32)
-    lane = lax.broadcasted_iota(jnp.int32, (members, obs), 1)
-    row = lax.broadcasted_iota(jnp.int32, (8, obs), 0)
-    lane8 = lax.broadcasted_iota(jnp.int32, (8, obs), 1)
-
-    def fetch(index, slot):
-        b, j = index // obs, index % obs
-        local = cell_s[b, j] - base
-        tile = pl.multiple_of(local // 128 * 128, 128)
-        return pltpu.make_async_copy(
-            x_hbm.at[stack_s[b, j], :, pl.ds(tile, 128)], buf.at[slot], sems.at[slot]
+def mate(index, step, size):
+    if size & (size - 1):
+        return lax.rem(index + step, size)
+    bit = 1
+    while bit <= step:
+        if step & bit:
+            index = index + bit - 2 * bit * (index // bit % 2)
+        bit *= 2
+    return index
+
+
+def column_of(row):
+    width = row.shape[1]
+    return jnp.transpose(jnp.broadcast_to(row, (128, width)))[:, 0:1]
+
+
+def gather_plan(gath, sends, receives):
+    rows, cols = lax.axis_size("row"), lax.axis_size("col")
+    plane = cols // 2
+    row, col = lax.axis_index("row"), lax.axis_index("col")
+    core, chip = lax.rem(col, 2), col // 2
+    other = (row, chip * 2 + 1 - core)
+
+    def near(step):
+        return (row, mate(chip, step, plane) * 2 + core)
+
+    def far(step):
+        return (mate(row, step, rows), col)
+
+    peers = [far(step) for step in range(1, rows)] + [near(step) for step in range(1, plane)] + [other]
+
+    def slot(row_step, chip_step, twin):
+        return (
+            mate(row, row_step, rows) * cols
+            + mate(chip, chip_step, plane) * 2
+            + (1 - core if twin else core)
         )
 
-    def group(number, carry):
-        first = number * SLOTS
-        held = jnp.minimum(count - first, SLOTS)
-
-        def start(slot, c):
-            fetch(found[first + slot], slot).start()
-            return c
-
-        def finish(slot, c):
-            index = found[first + slot]
-            fetch(index, slot).wait()
-            b, j = index // obs, index % obs
-            local = cell_s[b, j] - base
-            moved = pltpu.roll(buf[slot], (j - local % 128 + 128) % 128, axis=1)
-            top = pl.multiple_of(b * rows, 8)
-            acc[pl.ds(top, members), :] = jnp.where(
-                lane == j, moved, acc[pl.ds(top, members), :]
-            )
-            flag = jnp.where(row == 0, ocean_s[local].astype(jnp.float32), 0.0)
-            low = pl.multiple_of(top + members, 8)
-            acc[pl.ds(low, 8), :] = jnp.where(lane8 == j, flag, acc[pl.ds(low, 8), :])
-            return c
-
-        lax.fori_loop(0, held, start, 0)
-        lax.fori_loop(0, held, finish, 0)
-        return carry
-
-    lax.fori_loop(0, (count + SLOTS - 1) // SLOTS, group, 0)
-    for chunk in range(chunks):
-        out_ref[chunk] = acc[chunk * chunk_rows : (chunk + 1) * chunk_rows, :]
-
-
-def exchange_kernel(part, out, landed, send_a, recv_a, send_b, recv_b):
-    devices = part.shape[0]
-    cols = lax.axis_size("col")
-    me = device_number()
-
-    def peer(step):
-        return lax.rem(me + step, devices)
-
-    def place(number):
-        return (number // cols, lax.rem(number, cols))
-
-    barrier = pltpu.get_barrier_semaphore()
-
-    def greet(step, c):
-        pl.semaphore_signal(barrier, inc=1, device_id=place(peer(step)), device_id_type=MESH)
-        return c
-
-    lax.fori_loop(1, devices, greet, 0)
-    pl.semaphore_wait(barrier, devices - 1)
-
-    def scatter(other, slot):
-        return pltpu.make_async_remote_copy(
-            src_ref=part.at[other],
-            dst_ref=landed.at[slot],
-            send_sem=send_a.at[other],
-            recv_sem=recv_a.at[slot],
-            device_id=place(other),
+    started = []
+
+    def send(number, place):
+        copy = pltpu.make_async_remote_copy(
+            src_ref=gath.at[number],
+            dst_ref=gath.at[number],
+            send_sem=sends.at[len(started)],
+            recv_sem=receives.at[number],
+            device_id=place,
             device_id_type=MESH,
         )
-
-    def gather(other, slot):
-        return pltpu.make_async_remote_copy(
-            src_ref=out.at[me],
-            dst_ref=out.at[slot],
-            send_sem=send_b.at[other],
-            recv_sem=recv_b.at[slot],
-            device_id=place(other),
+        copy.start()
+        started.append(copy)
+
+    def arrive(number):
+        pltpu.make_async_remote_copy(
+            src_ref=gath.at[number],
+            dst_ref=gath.at[number],
+            send_sem=sends.at[0],
+            recv_sem=receives.at[number],
+            device_id=other,
             device_id_type=MESH,
+        ).wait_recv()
+
+    def spread(number):
+        for step in reversed(range(1, plane)):
+            send(number, near(step))
+        send(number, other)
+
+    def begin():
+        mine = slot(0, 0, False)
+        for step in reversed(range(1, rows)):
+            send(mine, far(step))
+        spread(mine)
+
+    def finish():
+        for step in range(1, rows):
+            number = slot(step, 0, False)
+            arrive(number)
+            spread(number)
+        for row_step in range(rows):
+            for step in range(1, plane):
+                number = slot(row_step, step, False)
+                arrive(number)
+                send(number, other)
+        for row_step in range(rows):
+            for step in range(plane):
+                arrive(slot(row_step, step, True))
+
+    def drain():
+        for copy in started:
+            copy.wait_send()
+
+    return peers, begin, finish, drain
+
+
+def share_kernel(
+    round_s,
+    ocean_s,
+    order_s,
+    order_ref,
+    cell_ref,
+    stack_ref,
+    x_hbm,
+    flat_ref,
+    rounds_s,
+    xt,
+    list_v,
+    list_s,
+    gath,
+    place_t,
+    sem_in,
+    sem_list,
+    sends,
+    receives,
+):
+    stack, members, columns = x_hbm.shape
+    batches, obs = cell_ref.shape
+    devices, cap, lanes = gath.shape
+    groups = columns // lanes
+    me = device_number()
+    state = [
+        pltpu.make_async_copy(
+            x_hbm.at[:, :, g * lanes : (g + 1) * lanes],
+            xt.at[g * stack : (g + 1) * stack],
+            sem_in.at[g],
         )
-
-    def each(act):
-        def step(number, c):
-            act(peer(number))
-            return c
-
-        lax.fori_loop(1, devices, step, 0)
-
-    each(lambda other: scatter(other, me).start())
-    landed[me] = part[me]
-    each(lambda other: scatter(other, other).wait_recv())
-    out[me] = jnp.sum(landed[...], axis=0)
-    each(lambda other: gather(other, me).start())
-    each(lambda other: gather(other, other).wait_recv())
-    each(lambda other: scatter(other, me).wait_send())
-    each(lambda other: gather(other, me).wait_send())
+        for g in range(groups)
+    ]
+    for copy in state:
+        copy.start()
+    peers, begin, finish, drain = gather_plan(gath, sends, receives)
+    barrier = pltpu.get_barrier_semaphore()
+    for place in peers:
+        pl.semaphore_signal(barrier, inc=1, device_id=place, device_id_type=MESH)
+
+    local = cell_ref[...] - order_s[me] * columns
+    here = jnp.logical_and(local >= 0, local < columns)
+    ahead = here.astype(jnp.int32)
+    total = ahead
+    along = lax.broadcasted_iota(jnp.int32, (batches, obs), 1)
+    step = 1
+    while step < obs:
+        ahead = ahead + jnp.where(along >= step, pltpu.roll(ahead, step, axis=1), 0)
+        total = total + pltpu.roll(total, step, axis=1)
+        step *= 2
+    code = stack_ref[...] * columns + local
+    slot_of = lax.broadcasted_iota(jnp.int32, (cap, obs), 0) + round_s[0] * cap + 1
+    codes = jnp.zeros((cap, obs), jnp.int32)
+    earlier = jnp.zeros((1, obs), jnp.int32)
+    for b in range(batches):
+        mine = jnp.where(here[b : b + 1], ahead[b : b + 1] + earlier, 0)
+        codes = codes + jnp.where(mine == slot_of, code[b : b + 1], 0)
+        earlier = earlier + total[b : b + 1]
+    step = 1
+    while step < obs:
+        codes = codes + pltpu.roll(codes, step, axis=1)
+        step *= 2
+    list_v[...] = codes
+    listing = pltpu.make_async_copy(list_v, list_s, sem_list)
+    listing.start()
+
+    first = (round_s[0] * cap).astype(jnp.float32)
+    number = lax.broadcasted_iota(jnp.int32, (devices, obs), 0).astype(jnp.float32)
+    square = (devices, devices)
+    same = lax.broadcasted_iota(jnp.int32, square, 0) == lax.broadcasted_iota(jnp.int32, square, 1)
+    order = jnp.sum(
+        jnp.where(same, order_ref[...].astype(jnp.float32), 0.0), axis=1, keepdims=True
+    )
+    before = lax.broadcasted_iota(jnp.int32, (obs, obs), 0) < lax.broadcasted_iota(
+        jnp.int32, (obs, obs), 1
+    )
+    before = before.astype(jnp.bfloat16)
+    count = jnp.zeros((devices, 1), jnp.float32)
+    slots = []
+    for b in range(batches):
+        cells = cell_ref[b : b + 1, :].astype(jnp.float32)
+        tile = jnp.floor((cells + 0.5) / columns)
+        holds = (order == tile).astype(jnp.float32)
+        rank = count + jnp.dot(
+            holds.astype(jnp.bfloat16), before, preferred_element_type=jnp.float32
+        )
+        count = count + jnp.sum(holds, axis=1, keepdims=True)
+        rank = jnp.sum(holds * rank, axis=0, keepdims=True) - first
+        holder = jnp.sum(holds * number, axis=0, keepdims=True)
+        now = jnp.logical_and(rank >= 0.0, rank < cap)
+        slots.append(jnp.where(now, holder * cap + rank, -1.0))
+    rounds_s[0] = jnp.max(jnp.floor((count + (cap - 0.5)) / cap)).astype(jnp.int32)
+    listing.wait()
+    for copy in state:
+        copy.wait()
+
+    lane = lax.broadcasted_iota(jnp.int32, (members, lanes), 1)
+    row8 = lax.broadcasted_iota(jnp.int32, (8, lanes), 0)
+    lane8 = lax.broadcasted_iota(jnp.int32, (8, lanes), 1)
+
+    def pick(k, carry):
+        held, flags = carry
+        code = list_s[k, 0]
+        level = lax.div(code, columns)
+        local = code - level * columns
+        group = lax.div(local, lanes)
+        block = xt[group * stack + level]
+        moved = pltpu.roll(block, lax.rem(k - (local - group * lanes) + lanes, lanes), axis=1)
+        held = jnp.where(lane == k, moved, held)
+        flag = jnp.where(row8 == 0, ocean_s[local].astype(jnp.float32), 0.0)
+        return held, jnp.where(lane8 == k, flag, flags)
+
+    held, flags = lax.fori_loop(
+        0,
+        cap,
+        pick,
+        (jnp.zeros((members, lanes), jnp.float32), jnp.zeros((8, lanes), jnp.float32)),
+        unroll=8,
+    )
+    rest = jnp.zeros((lanes - members - 8, lanes), jnp.float32)
+    gath[me] = jnp.transpose(jnp.concatenate([held, flags, rest], axis=0))[0:cap, :]
+
+    pl.semaphore_wait(barrier, len(peers))
+    begin()
+    at = lax.broadcasted_iota(jnp.int32, (obs, devices * cap), 1).astype(jnp.float32)
+    for b in range(batches):
+        place_t[b * obs : (b + 1) * obs, :] = (column_of(slots[b]) == at).astype(jnp.bfloat16)
+    finish()
+
+    got = jnp.concatenate([gath[k] for k in range(devices)], axis=0)
+    high, low = split(got)
+    rest = (got - high.astype(jnp.float32) - low.astype(jnp.float32)).astype(jnp.bfloat16)
+    parts = jnp.dot(
+        place_t[...],
+        jnp.concatenate([high, low, rest], axis=1),
+        preferred_element_type=jnp.float32,
+    )
+    placed = parts[:, 0:lanes] + parts[:, lanes : 2 * lanes] + parts[:, 2 * lanes :]
+    for b in range(batches):
+        flat_ref[b] = jnp.transpose(placed[b * obs : (b + 1) * obs, :])
+    drain()
 
 
 def split(values):
@@ -163,7 +280,6 @@
 
 
 def update_kernel(
-    rows,
     order_s,
     ocean_ref,
     cell_ref,
@@ -176,7 +292,6 @@
     x_hbm,
     y_hbm,
     xt,
-    flat,
     side_a,
     side_d,
     lhs_a,
@@ -187,7 +302,6 @@
 ):
     stack, members, columns = xt.shape
     batches, obs = cell_ref.shape
-    chunks, chunk_rows, _ = shared_ref.shape
 
     def incoming(v):
         return pltpu.make_async_copy(x_hbm.at[v], xt.at[v], sem_in.at[v])
@@ -201,16 +315,14 @@
 
     lax.fori_loop(0, stack, begin, 0)
 
-    for chunk in range(chunks):
-        flat[chunk * chunk_rows : (chunk + 1) * chunk_rows, :] = shared_ref[chunk]
     base = (order_s[device_number()] * columns).astype(jnp.float32)
     places = base + lax.broadcasted_iota(jnp.int32, (1, columns), 1).astype(jnp.float32)
     ocean = ocean_ref[...].astype(jnp.float32)
     cells = cell_ref[...].astype(jnp.float32)
     starts = start_ref[...].astype(jnp.float32)
     ends = (start_ref[...] + span_ref[...]).astype(jnp.float32)
-    priors = [flat[b * rows : b * rows + members, :] for b in range(batches)]
-    flags = [flat[b * rows + members : b * rows + members + 1, :] for b in range(batches)]
+    priors = [shared_ref[b, 0:members, :] for b in range(batches)]
+    flags = [shared_ref[b, members : members + 1, :] for b in range(batches)]
     scale = 1.0 / (members - 1.0)
     meets = jnp.logical_and(starts < base + columns, ends > base).astype(jnp.float32)
     before = lax.broadcasted_iota(jnp.int32, (obs, obs), 0) < lax.broadcasted_iota(
@@ -344,48 +456,52 @@
     members, stack, columns = prior.shape
     batches, obs = obs_cell.shape
     devices = tile_order.shape[0]
-    rows = members + 8
-    chunk_rows = -(-batches * rows // devices)
+    mean = -(-batches * obs // devices)
+    cap = min(round_up(mean + 4 * math.isqrt(mean), 8), 128)
     smem = pl.BlockSpec(memory_space=pltpu.SMEM)
     vmem = pl.BlockSpec(memory_space=pltpu.VMEM)
     hbm = pl.BlockSpec(memory_space=pl.ANY)
-    shared_shape = jax.ShapeDtypeStruct((devices, chunk_rows, obs), jnp.float32)
-    flat_rows = round_up(devices * chunk_rows, 8)
 
     levels = jnp.transpose(prior, (1, 0, 2))
-    part = pl.pallas_call(
-        functools.partial(extract_kernel, columns, rows),
-        out_shape=shared_shape,
-        in_specs=[smem, smem, smem, smem, hbm],
-        out_specs=vmem,
-        scratch_shapes=[
-            pltpu.SMEM((batches * obs + 1,), jnp.int32),
-            pltpu.VMEM((SLOTS, members, 128), jnp.float32),
-            pltpu.VMEM((flat_rows, obs), jnp.float32),
-            pltpu.SemaphoreType.DMA((SLOTS,)),
-        ],
-        name="extract",
-    )(tile_order, obs_cell, obs_stack, ocean_mask, levels)
-
-    shared = pl.pallas_call(
-        exchange_kernel,
-        out_shape=shared_shape,
-        in_specs=[vmem],
-        out_specs=vmem,
-        scratch_shapes=[pltpu.VMEM((devices, chunk_rows, obs), jnp.float32)]
-        + [pltpu.SemaphoreType.DMA((devices,))] * 4,
-        compiler_params=pltpu.CompilerParams(collective_id=0, has_side_effects=True),
-        name="exchange",
-    )(part)
+
+    def share(number):
+        return pl.pallas_call(
+            share_kernel,
+            out_shape=(
+                jax.ShapeDtypeStruct((batches, 128, obs), jnp.float32),
+                jax.ShapeDtypeStruct((1,), jnp.int32),
+            ),
+            in_specs=[smem, smem, smem, vmem, vmem, vmem, hbm],
+            out_specs=(vmem, smem),
+            scratch_shapes=[
+                pltpu.VMEM((columns // 128 * stack, members, 128), jnp.float32),
+                pltpu.VMEM((cap, obs), jnp.int32),
+                pltpu.SMEM((cap, obs), jnp.int32),
+                pltpu.VMEM((devices, cap, 128), jnp.float32),
+                pltpu.VMEM((batches * obs, devices * cap), jnp.bfloat16),
+                pltpu.SemaphoreType.DMA((columns // 128,)),
+                pltpu.SemaphoreType.DMA,
+                pltpu.SemaphoreType.DMA((devices,)),
+                pltpu.SemaphoreType.DMA((devices,)),
+            ],
+            compiler_params=pltpu.CompilerParams(collective_id=0, has_side_effects=True),
+            name="share",
+        )(number, ocean_mask, tile_order, tile_order.reshape(1, devices), obs_cell, obs_stack, levels)
+
+    shared, rounds = share(jnp.zeros((1,), jnp.int32))
+    _, shared = lax.while_loop(
+        lambda carry: carry[0] < rounds[0],
+        lambda carry: (carry[0] + 1, carry[1] + share(carry[0].reshape(1))[0]),
+        (jnp.int32(1), shared),
+    )
 
     updated = pl.pallas_call(
-        functools.partial(update_kernel, rows),
+        update_kernel,
         out_shape=jax.ShapeDtypeStruct(levels.shape, levels.dtype),
         in_specs=[smem] + [vmem] * 8 + [hbm],
         out_specs=hbm,
         scratch_shapes=[
             pltpu.VMEM((stack, members, columns), jnp.float32),
-            pltpu.VMEM((flat_rows, obs), jnp.float32),
             pltpu.VMEM((batches, 3 * members, obs), jnp.bfloat16),
             pltpu.VMEM((batches, 2, members, obs), jnp.bfloat16),
             pltpu.VMEM((batches, obs, 3 * members), jnp.bfloat16),

time: 42.5 us -> 32.8 us (0.77); the launches traced: 41.8 us -> 32.6 us
  Pallas kernels: 41.8 us -> 31.9 us
  loops' own time: 0 us -> 0.64 us
    pallas_call x3 -> x2, Pallas kernels: 41.8 us -> 31.9 us  [the longest x1 17.8 us: share(): pl.pallas_call(share_kernel, out_shape=(jax.ShapeDtypeStruct((batches, 12...]
    another operation x0 -> x1, loops' own time: none -> 0.64 us  [per_device(): lax.while_loop(lambda carry: carry[0] < rounds[0], lambda carry: (carry[0...]
where the time goes in v2:
time: 32.8 us; the launch traced here: 32.6 us
  Pallas kernels  31.9 us (97%)
  loops' own time  0.64 us (2%)
    pallas_call x1, Pallas kernels, share(): pl.pallas_call(share_kernel, out_shape=(jax.ShapeDtypeStruct((batches, 12...  17.8 us
    pallas_call x1, Pallas kernels, per_device(): pl.pallas_call(update_kernel, out_shape=jax.ShapeDtypeStruct(levels.shape...  14.1 us

profile of v2, /device:TPU:1, one launch (start us, length us, event | category | flops | bytes accessed | tf_op | source)
XLA Modules:
  0.0 32.6 jit_solution(15976471934166619163)
XLA Ops:
  0.0 0.0 copy-start.2
  0.0 0.0 copy-start.1
  0.0 0.0 copy-start
  0.0 0.0 copy-start.3
  0.0 17.8 %share.2 = (f32[4,128,128]{2,1,0:T(8,128)S(1)}, s32[1]{0:T(128)}) custom-call(s32[1]{0:T(128)} %constant.2.clone.1.round_s, s32[512]{0:T(512)} %ocean_s.1, s32[32]{0:T(128)} %order_s.3, s32[1,32]{1,0:T(1,128)} %bitcast.15, s32[4,128]{1,0:T(4,128)} %cell_ref.3, s32[4,128]{1,0:T(4,128)} %stack_ref.1, f32[30,80,512]{2,1,0:T(8,128)} %bitcast.12), custom_call_target="tpu_custom_call" | custom-call | tf_op jit(solution)/shard_map/share/pallas_call | solution.py:468
  17.8 0.0 copy-done.2
  17.8 0.0 copy-done.1
  17.8 0.0 copy-done
  17.8 0.0 copy-done.3
  17.9 0.6 %while.10 = (s32[]{:T(128)}, f32[4,128,128]{2,1,0:T(8,128)S(1)}, s32[1]{0:T(128)}, s32[32]{0:T(128)S(1)}, s32[512]{0:T(512)S(1)}, /*index=5*/s32[4,128]{1,0:T(4,...) while((s32[]{:T(128)}, f32[4,128,128]{2,1,0:T(8,128)S(1)}, s32[1]{0:T(128)}, s32[32]{0:T(128)S(1)}, ...), condition=%wide.region_1.0_spmd, body=%wide.region_0.0_spmd.sunk | while | flops 65538 | bytes 786533 | solution.py:492
  18.5 14.1 %update.1 = f32[30,80,512]{2,1,0:T(8,128)} custom-call(s32[32]{0:T(128)S(1)} %get-tuple-element.152, s32[1,512]{1,0:T(1,128)S(1)} %bitcast.14, s32[4,128]{1,0:T(4,128)S(1)} %get-tuple-element.151, s32[4,128]{1,0:T(4,128)} %start_ref.1, s32[4,128]{1,0:T(4,128)} %span_ref.1, f32[4,128]{1,0:T(4,128)} %value_ref.1, f32[4,128,128]{2,1,0:T(8,128)} %mean_ref.1, ...), custom_call_target="tpu_custom_call" | custom-call | tf_op jit(solution)/shard_map/update/pallas_call | solution.py:498
Async XLA Ops:
  0.0 17.8 %copy-start.2 = (s32[32]{0:T(128)S(1)}, s32[32]{0:T(128)}, u32[]{:S(2)}) copy-start(s32[32]{0:T(128)} %order_s.3) | copy-start | bytes 388
  0.0 17.8 %copy-start.1 = (s32[4,128]{1,0:T(4,128)S(1)}, s32[4,128]{1,0:T(4,128)}, u32[]{:S(2)}) copy-start(s32[4,128]{1,0:T(4,128)} %cell_ref.3) | copy-start | bytes 6148
  0.0 17.8 %copy-start = (s32[512]{0:T(512)S(1)}, s32[512]{0:T(512)}, u32[]{:S(2)}) copy-start(s32[512]{0:T(512)} %ocean_s.1) | copy-start | bytes 6148
  0.0 17.8 %copy-start.3 = (s32[4,128]{1,0:T(4,128)S(1)}, s32[4,128]{1,0:T(4,128)}, u32[]{:S(2)}) copy-start(s32[4,128]{1,0:T(4,128)} %stack_ref.1) | copy-start | bytes 6148

commit v3 on v2

--- a/solution.py
+++ b/solution.py
@@ -30,6 +30,10 @@
             index = index + bit - 2 * bit * (index // bit % 2)
         bit *= 2
     return index
+
+
+def most_levels(stack, limit):
+    return max(k for k in range(1, limit + 1) if stack % k == 0)
 
 
 def column_of(row):
@@ -297,6 +301,7 @@
     lhs_a,
     lhs_d,
     weight,
+    held,
     sem_in,
     sem_out,
 ):
@@ -373,10 +378,10 @@
             for a in range(b + 1, batches):
                 priors[a] = later[:, (a - b - 1) * obs : (a - b) * obs]
 
-    together = max(k for k in range(1, 7) if stack % k == 0)
-
     def sweep_with(kept):
+        together = most_levels(stack, held.shape[0] if kept == min(SIZES) else 5)
         slot = lax.broadcasted_iota(jnp.int32, (kept, obs), 0).astype(jnp.float32)
+        before_d = None
         for b in range(batches):
             chosen = jnp.logical_and(slot == ranks[b : b + 1], meets[b : b + 1] > 0.0)
             start_of = jnp.sum(jnp.where(chosen, starts[b : b + 1], 0.0), axis=1, keepdims=True)
@@ -385,42 +390,64 @@
                 jnp.logical_and(places >= start_of, places < end_of), ocean, 0.0
             )
             pick = chosen.astype(jnp.bfloat16)
-            none = jnp.zeros_like(pick)
-            lhs_a[b, 0:kept] = lax.dot_general(
+            second = b % 2
+            rows = slice(second * kept, second * kept + kept)
+            lhs_a[b // 2, rows] = lax.dot_general(
                 pick, side_a[b], NT, preferred_element_type=jnp.float32
             ).astype(jnp.bfloat16)
-            lhs_d[b, :, 0 : 3 * kept] = (
-                lax.dot_general(
-                    side_d[b, 0],
-                    jnp.concatenate([pick, pick, none], axis=0),
-                    NT,
+            highs = lax.dot_general(side_d[b, 0], pick, NT, preferred_element_type=jnp.float32)
+            lows = lax.dot_general(side_d[b, 1], pick, NT, preferred_element_type=jnp.float32)
+            parts = jnp.concatenate([highs, highs, lows], axis=1).astype(jnp.bfloat16)
+            lhs_d[b, 0:members, 0 : 3 * kept] = parts
+            if second:
+                cross = jnp.dot(
+                    lhs_a[b // 2, rows],
+                    before_d,
                     preferred_element_type=jnp.float32,
                 )
-                + lax.dot_general(
-                    side_d[b, 1],
-                    jnp.concatenate([none, none, pick], axis=0),
-                    NT,
-                    preferred_element_type=jnp.float32,
-                )
-            ).astype(jnp.bfloat16)
+                c_high, c_low = split(cross)
+                lhs_d[b - 1, members : members + kept, 0 : 3 * kept] = jnp.concatenate([c_high, c_high, c_low], axis=1)
+            else:
+                before_d = jnp.concatenate([highs, lows, highs], axis=0).astype(jnp.bfloat16)
 
         def sweep(number, c):
             levels = [number * together + k for k in range(together)]
             for v in levels:
                 incoming(v).wait()
             values = [xt[v] for v in levels]
-            for b in range(batches):
-                gains = []
+            for b in range(0, batches, 2):
+                both = []
                 for k in range(together):
-                    gain = weight[b, 0:kept] * jnp.dot(
-                        lhs_a[b, 0:kept],
-                        triple(values[k], 0),
-                        preferred_element_type=jnp.float32,
+                    both.append(
+                        jnp.dot(
+                            lhs_a[b // 2, 0 : 2 * kept],
+                            triple(values[k], 0),
+                            preferred_element_type=jnp.float32,
+                        )
                     )
-                    gains.append(triple(gain, 0))
                 for k in range(together):
-                    values[k] = values[k] + jnp.dot(
-                        lhs_d[b, :, 0 : 3 * kept], gains[k], preferred_element_type=jnp.float32
+                    held[k, 0:kept] = both[k][kept:]
+                moved = []
+                for k in range(together):
+                    gain = triple(weight[b, 0:kept] * both[k][0:kept], 0)
+                    moved.append(
+                        jnp.dot(
+                            lhs_d[b, 0 : kept + members, 0 : 3 * kept],
+                            gain,
+                            preferred_element_type=jnp.float32,
+                        )
+                    )
+                for k in range(together):
+                    xt[levels[k]] = values[k] + moved[k][0:members]
+                for k in range(together):
+                    gain = weight[b + 1, 0:kept] * (held[k, 0:kept] + moved[k][members:])
+                    values[k] = (
+                        xt[levels[k]]
+                        + jnp.dot(
+                            lhs_d[b + 1, 0:members, 0 : 3 * kept],
+                            triple(gain, 0),
+                            preferred_element_type=jnp.float32,
+                        )
                     )
             for k in range(together):
                 xt[levels[k]] = values[k]
@@ -504,9 +531,10 @@
             pltpu.VMEM((stack, members, columns), jnp.float32),
             pltpu.VMEM((batches, 3 * members, obs), jnp.bfloat16),
             pltpu.VMEM((batches, 2, members, obs), jnp.bfloat16),
-            pltpu.VMEM((batches, obs, 3 * members), jnp.bfloat16),
-            pltpu.VMEM((batches, members, 3 * obs), jnp.bfloat16),
+            pltpu.VMEM((batches // 2, 2 * obs, 3 * members), jnp.bfloat16),
+            pltpu.VMEM((batches, members + obs, 3 * obs), jnp.bfloat16),
             pltpu.VMEM((batches, obs, columns), jnp.float32),
+            pltpu.VMEM((most_levels(stack, 10), obs, columns), jnp.float32),
             pltpu.SemaphoreType.DMA((stack,)),
             pltpu.SemaphoreType.DMA((stack,)),
         ],

time: 32.8 us -> 30.2 us (0.921)
  Pallas kernels: 31.9 us -> 29.4 us
    pallas_call x1, Pallas kernels: 14.1 us -> 11.6 us  [per_device(): pl.pallas_call(update_kernel, out_shape=jax.ShapeDtypeStruct(levels.shape...]
where the time goes in v3:
time: 30.2 us; the launch traced here: 30.1 us
  Pallas kernels  29.4 us (97%)
  loops' own time  0.64 us (2%)
    pallas_call x1, Pallas kernels, share(): pl.pallas_call(share_kernel, out_shape=(jax.ShapeDtypeStruct((batches, 12...  17.8 us
    pallas_call x1, Pallas kernels, per_device(): pl.pallas_call(update_kernel, out_shape=jax.ShapeDtypeStruct(levels.shape...  11.6 us
    another operation x1, loops' own time, per_device(): lax.while_loop(lambda carry: carry[0] < rounds[0], lambda carry: (carry[0...  0.64 us

profile of v3, /device:TPU:1, one launch (start us, length us, event | category | flops | bytes accessed | tf_op | source)
XLA Modules:
  0.0 30.1 jit_solution(3028997772501571017)
XLA Ops:
  0.0 0.0 copy-start.2
  0.0 0.0 copy-start.1
  0.0 0.0 copy-start
  0.0 0.0 copy-start.3
  0.0 17.8 %share.2 = (f32[4,128,128]{2,1,0:T(8,128)S(1)}, s32[1]{0:T(128)}) custom-call(s32[1]{0:T(128)} %constant.2.clone.1.round_s, s32[512]{0:T(512)} %ocean_s.1, s32[32]{0:T(128)} %order_s.3, s32[1,32]{1,0:T(1,128)} %bitcast.15, s32[4,128]{1,0:T(4,128)} %cell_ref.3, s32[4,128]{1,0:T(4,128)} %stack_ref.1, f32[30,80,512]{2,1,0:T(8,128)} %bitcast.12), custom_call_target="tpu_custom_call" | custom-call | tf_op jit(solution)/shard_map/share/pallas_call | solution.py:495
  17.8 0.0 copy-done.2
  17.8 0.0 copy-done.1
  17.8 0.0 copy-done
  17.8 0.0 copy-done.3
  17.9 0.6 %while.10 = (s32[]{:T(128)}, f32[4,128,128]{2,1,0:T(8,128)S(1)}, s32[1]{0:T(128)}, s32[32]{0:T(128)S(1)}, s32[512]{0:T(512)S(1)}, /*index=5*/s32[4,128]{1,0:T(4,...) while((s32[]{:T(128)}, f32[4,128,128]{2,1,0:T(8,128)S(1)}, s32[1]{0:T(128)}, s32[32]{0:T(128)S(1)}, ...), condition=%wide.region_1.0_spmd, body=%wide.region_0.0_spmd.sunk | while | flops 65538 | bytes 786533 | solution.py:519
  18.5 11.6 %update.1 = f32[30,80,512]{2,1,0:T(8,128)} custom-call(s32[32]{0:T(128)S(1)} %get-tuple-element.152, s32[1,512]{1,0:T(1,128)S(1)} %bitcast.14, s32[4,128]{1,0:T(4,128)S(1)} %get-tuple-element.151, s32[4,128]{1,0:T(4,128)} %start_ref.1, s32[4,128]{1,0:T(4,128)} %span_ref.1, f32[4,128]{1,0:T(4,128)} %value_ref.1, f32[4,128,128]{2,1,0:T(8,128)} %mean_ref.1, ...), custom_call_target="tpu_custom_call" | custom-call | tf_op jit(solution)/shard_map/update/pallas_call | solution.py:525
Async XLA Ops:
  0.0 17.8 %copy-start.2 = (s32[32]{0:T(128)S(1)}, s32[32]{0:T(128)}, u32[]{:S(2)}) copy-start(s32[32]{0:T(128)} %order_s.3) | copy-start | bytes 388
  0.0 17.8 %copy-start.1 = (s32[4,128]{1,0:T(4,128)S(1)}, s32[4,128]{1,0:T(4,128)}, u32[]{:S(2)}) copy-start(s32[4,128]{1,0:T(4,128)} %cell_ref.3) | copy-start | bytes 6148
  0.0 17.8 %copy-start = (s32[512]{0:T(512)S(1)}, s32[512]{0:T(512)}, u32[]{:S(2)}) copy-start(s32[512]{0:T(512)} %ocean_s.1) | copy-start | bytes 6148
  0.0 17.8 %copy-start.3 = (s32[4,128]{1,0:T(4,128)S(1)}, s32[4,128]{1,0:T(4,128)}, u32[]{:S(2)}) copy-start(s32[4,128]{1,0:T(4,128)} %stack_ref.1) | copy-start | bytes 6148

commit v4 on v3

--- a/solution.py
+++ b/solution.py
@@ -36,42 +36,34 @@
     return max(k for k in range(1, limit + 1) if stack % k == 0)
 
 
-def column_of(row):
-    width = row.shape[1]
-    return jnp.transpose(jnp.broadcast_to(row, (128, width)))[:, 0:1]
-
-
 def gather_plan(gath, sends, receives):
     rows, cols = lax.axis_size("row"), lax.axis_size("col")
     plane = cols // 2
     row, col = lax.axis_index("row"), lax.axis_index("col")
     core, chip = lax.rem(col, 2), col // 2
     other = (row, chip * 2 + 1 - core)
-
-    def near(step):
-        return (row, mate(chip, step, plane) * 2 + core)
-
-    def far(step):
-        return (mate(row, step, rows), col)
-
-    peers = [far(step) for step in range(1, rows)] + [near(step) for step in range(1, plane)] + [other]
-
-    def slot(row_step, chip_step, twin):
+    steps = [(a, b) for a in range(rows) for b in range(plane) if a or b]
+    steps.sort(key=lambda step: step[0] + step[1].bit_count())
+
+    def place(step):
+        return (mate(row, step[0], rows), mate(chip, step[1], plane) * 2 + core)
+
+    def slot(step, twin):
         return (
-            mate(row, row_step, rows) * cols
-            + mate(chip, chip_step, plane) * 2
+            mate(row, step[0], rows) * cols
+            + mate(chip, step[1], plane) * 2
             + (1 - core if twin else core)
         )
 
     started = []
 
-    def send(number, place):
+    def send(number, to):
         copy = pltpu.make_async_remote_copy(
             src_ref=gath.at[number],
             dst_ref=gath.at[number],
             send_sem=sends.at[len(started)],
             recv_sem=receives.at[number],
-            device_id=place,
+            device_id=to,
             device_id_type=MESH,
         )
         copy.start()
@@ -87,36 +79,25 @@
             device_id_type=MESH,
         ).wait_recv()
 
-    def spread(number):
-        for step in reversed(range(1, plane)):
-            send(number, near(step))
-        send(number, other)
-
     def begin():
-        mine = slot(0, 0, False)
-        for step in reversed(range(1, rows)):
-            send(mine, far(step))
-        spread(mine)
+        mine = slot((0, 0), False)
+        for step in reversed(steps):
+            send(mine, place(step))
+        send(mine, other)
 
     def finish():
-        for step in range(1, rows):
-            number = slot(step, 0, False)
+        for step in steps:
+            number = slot(step, False)
             arrive(number)
-            spread(number)
-        for row_step in range(rows):
-            for step in range(1, plane):
-                number = slot(row_step, step, False)
-                arrive(number)
-                send(number, other)
-        for row_step in range(rows):
-            for step in range(plane):
-                arrive(slot(row_step, step, True))
+            send(number, other)
+        for step in [(0, 0)] + steps:
+            arrive(slot(step, True))
 
     def drain():
         for copy in started:
             copy.wait_send()
 
-    return peers, begin, finish, drain
+    return [place(step) for step in steps] + [other], begin, finish, drain
 
 
 def share_kernel(
@@ -133,7 +114,7 @@
     list_v,
     list_s,
     gath,
-    place_t,
+    one_hot,
     sem_in,
     sem_list,
     sends,
@@ -141,8 +122,10 @@
 ):
     stack, members, columns = x_hbm.shape
     batches, obs = cell_ref.shape
-    devices, cap, lanes = gath.shape
+    devices, piece, lanes = gath.shape
+    cap = one_hot.shape[0] // devices
     groups = columns // lanes
+    parts = lanes // cap
     me = device_number()
     state = [
         pltpu.make_async_copy(
@@ -181,7 +164,12 @@
     while step < obs:
         codes = codes + pltpu.roll(codes, step, axis=1)
         step *= 2
-    list_v[...] = codes
+    diagonal = lax.broadcasted_iota(jnp.int32, (cap, obs), 0) == lax.broadcasted_iota(
+        jnp.int32, (cap, obs), 1
+    )
+    list_v[...] = jnp.broadcast_to(
+        jnp.sum(jnp.where(diagonal, codes, 0), axis=0, keepdims=True), list_v.shape
+    )
     listing = pltpu.make_async_copy(list_v, list_s, sem_list)
     listing.start()
 
@@ -221,7 +209,7 @@
 
     def pick(k, carry):
         held, flags = carry
-        code = list_s[k, 0]
+        code = list_s[0, k]
         level = lax.div(code, columns)
         local = code - level * columns
         group = lax.div(local, lanes)
@@ -238,27 +226,42 @@
         (jnp.zeros((members, lanes), jnp.float32), jnp.zeros((8, lanes), jnp.float32)),
         unroll=8,
     )
-    rest = jnp.zeros((lanes - members - 8, lanes), jnp.float32)
-    gath[me] = jnp.transpose(jnp.concatenate([held, flags, rest], axis=0))[0:cap, :]
+    rest = jnp.zeros((parts * piece - members - 8, lanes), jnp.float32)
+    held = jnp.concatenate([held, flags, rest], axis=0)
+    part_of = lax.broadcasted_iota(jnp.int32, (piece, lanes), 1) // cap
+    packed = held[0:piece]
+    for g in range(1, parts):
+        moved = pltpu.roll(held[g * piece : (g + 1) * piece], g * cap, axis=1)
+        packed = jnp.where(part_of == g, moved, packed)
+    gath[me] = packed
 
     pl.semaphore_wait(barrier, len(peers))
     begin()
-    at = lax.broadcasted_iota(jnp.int32, (obs, devices * cap), 1).astype(jnp.float32)
+    at = lax.broadcasted_iota(jnp.int32, (devices * cap, obs), 0).astype(jnp.float32)
     for b in range(batches):
-        place_t[b * obs : (b + 1) * obs, :] = (column_of(slots[b]) == at).astype(jnp.bfloat16)
+        one_hot[:, b * obs : (b + 1) * obs] = (slots[b] == at).astype(jnp.bfloat16)
     finish()
 
-    got = jnp.concatenate([gath[k] for k in range(devices)], axis=0)
-    high, low = split(got)
-    rest = (got - high.astype(jnp.float32) - low.astype(jnp.float32)).astype(jnp.bfloat16)
-    parts = jnp.dot(
-        place_t[...],
-        jnp.concatenate([high, low, rest], axis=1),
-        preferred_element_type=jnp.float32,
-    )
-    placed = parts[:, 0:lanes] + parts[:, lanes : 2 * lanes] + parts[:, 2 * lanes :]
+    unpacked = []
+    for g in range(parts):
+        tiles = []
+        for first_device in range(0, devices, parts):
+            tile = None
+            for q in range(parts):
+                moved = gath[first_device + q]
+                if q != g:
+                    moved = pltpu.roll(moved, (q - g) % parts * cap, axis=1)
+                tile = moved if q == 0 else jnp.where(part_of == q, moved, tile)
+            tiles.append(tile)
+        unpacked.append(jnp.concatenate(tiles, axis=1))
+    high, low = split(jnp.concatenate(unpacked, axis=0))
+    placed = jnp.dot(
+        jnp.concatenate([high, low], axis=0), one_hot[...], preferred_element_type=jnp.float32
+    )
+    height = parts * piece
+    placed = placed[0:height] + placed[height:]
     for b in range(batches):
-        flat_ref[b] = jnp.transpose(placed[b * obs : (b + 1) * obs, :])
+        flat_ref[b] = placed[:, b * obs : (b + 1) * obs]
     drain()
 
 
@@ -484,7 +487,11 @@
     batches, obs = obs_cell.shape
     devices = tile_order.shape[0]
     mean = -(-batches * obs // devices)
-    cap = min(round_up(mean + 4 * math.isqrt(mean), 8), 128)
+    cap = 8
+    while cap < min(mean + 4 * math.isqrt(mean), 128):
+        cap *= 2
+    parts = 128 // cap
+    piece = round_up(-(-(members + 8) // parts), 8)
     smem = pl.BlockSpec(memory_space=pltpu.SMEM)
     vmem = pl.BlockSpec(memory_space=pltpu.VMEM)
     hbm = pl.BlockSpec(memory_space=pl.ANY)
@@ -495,17 +502,17 @@
         return pl.pallas_call(
             share_kernel,
             out_shape=(
-                jax.ShapeDtypeStruct((batches, 128, obs), jnp.float32),
+                jax.ShapeDtypeStruct((batches, parts * piece, obs), jnp.float32),
                 jax.ShapeDtypeStruct((1,), jnp.int32),
             ),
             in_specs=[smem, smem, smem, vmem, vmem, vmem, hbm],
             out_specs=(vmem, smem),
             scratch_shapes=[
                 pltpu.VMEM((columns // 128 * stack, members, 128), jnp.float32),
-                pltpu.VMEM((cap, obs), jnp.int32),
-                pltpu.SMEM((cap, obs), jnp.int32),
-                pltpu.VMEM((devices, cap, 128), jnp.float32),
-                pltpu.VMEM((batches * obs, devices * cap), jnp.bfloat16),
+                pltpu.VMEM((1, obs), jnp.int32),
+                pltpu.SMEM((1, obs), jnp.int32),
+                pltpu.VMEM((devices, piece, 128), jnp.float32),
+                pltpu.VMEM((devices * cap, batches * obs), jnp.bfloat16),
                 pltpu.SemaphoreType.DMA((columns // 128,)),
                 pltpu.SemaphoreType.DMA,
                 pltpu.SemaphoreType.DMA((devices,)),

time: 30.2 us -> 29 us (0.960)
  Pallas kernels: 29.4 us -> 28.1 us
    pallas_call x1, Pallas kernels: 17.8 us -> 16.5 us  [share(): pl.pallas_call(share_kernel, out_shape=(jax.ShapeDtypeStruct((batches, pa...]
where the time goes in v4:
time: 29 us; the launch traced here: 28.9 us
  Pallas kernels  28.1 us (97%)
  loops' own time  0.69 us (2%)
    pallas_call x1, Pallas kernels, share(): pl.pallas_call(share_kernel, out_shape=(jax.ShapeDtypeStruct((batches, pa...  16.5 us
    pallas_call x1, Pallas kernels, per_device(): pl.pallas_call(update_kernel, out_shape=jax.ShapeDtypeStruct(levels.shape...  11.6 us
    another operation x1, loops' own time, per_device(): lax.while_loop(lambda carry: carry[0] < rounds[0], lambda carry: (carry[0...  0.69 us

profile of v4, /device:TPU:1, one launch (start us, length us, event | category | flops | bytes accessed | tf_op | source)
XLA Modules:
  0.0 28.9 jit_solution(8244917281710918293)
XLA Ops:
  0.0 0.0 copy-start.2
  0.0 0.0 copy-start.1
  0.0 0.0 copy-start
  0.0 0.0 copy-start.3
  0.0 16.5 %share.2 = (f32[4,96,128]{2,1,0:T(8,128)S(1)}, s32[1]{0:T(128)}) custom-call(s32[1]{0:T(128)} %constant.2.clone.1.round_s, s32[512]{0:T(512)} %ocean_s.1, s32[32]{0:T(128)} %order_s.3, s32[1,32]{1,0:T(1,128)} %bitcast.15, s32[4,128]{1,0:T(4,128)} %cell_ref.3, s32[4,128]{1,0:T(4,128)} %stack_ref.1, f32[30,80,512]{2,1,0:T(8,128)} %bitcast.12), custom_call_target="tpu_custom_call" | custom-call | tf_op jit(solution)/shard_map/share/pallas_call | solution.py:502
  16.5 0.0 copy-done.2
  16.5 0.0 copy-done.1
  16.5 0.0 copy-done
  16.5 0.0 copy-done.3
  16.5 0.7 %while.10 = (s32[]{:T(128)}, f32[4,96,128]{2,1,0:T(8,128)S(1)}, s32[1]{0:T(128)}, s32[32]{0:T(128)S(1)}, s32[512]{0:T(512)S(1)}, /*index=5*/s32[4,128]{1,0:T(4,1...) while((s32[]{:T(128)}, f32[4,96,128]{2,1,0:T(8,128)S(1)}, s32[1]{0:T(128)}, s32[32]{0:T(128)S(1)}, ...), condition=%wide.region_1.0_spmd, body=%wide.region_0.0_spmd.sunk | while | flops 49154 | bytes 589925 | solution.py:526
  17.2 11.6 %update.1 = f32[30,80,512]{2,1,0:T(8,128)} custom-call(s32[32]{0:T(128)S(1)} %get-tuple-element.152, s32[1,512]{1,0:T(1,128)S(1)} %bitcast.14, s32[4,128]{1,0:T(4,128)S(1)} %get-tuple-element.151, s32[4,128]{1,0:T(4,128)} %start_ref.1, s32[4,128]{1,0:T(4,128)} %span_ref.1, f32[4,128]{1,0:T(4,128)} %value_ref.1, f32[4,128,128]{2,1,0:T(8,128)} %mean_ref.1, ...), custom_call_target="tpu_custom_call" | custom-call | tf_op jit(solution)/shard_map/update/pallas_call | solution.py:532
Async XLA Ops:
  0.0 16.5 %copy-start.2 = (s32[32]{0:T(128)S(1)}, s32[32]{0:T(128)}, u32[]{:S(2)}) copy-start(s32[32]{0:T(128)} %order_s.3) | copy-start | bytes 388
  0.0 16.5 %copy-start.1 = (s32[4,128]{1,0:T(4,128)S(1)}, s32[4,128]{1,0:T(4,128)}, u32[]{:S(2)}) copy-start(s32[4,128]{1,0:T(4,128)} %cell_ref.3) | copy-start | bytes 6148
  0.0 16.5 %copy-start = (s32[512]{0:T(512)S(1)}, s32[512]{0:T(512)}, u32[]{:S(2)}) copy-start(s32[512]{0:T(512)} %ocean_s.1) | copy-start | bytes 6148
  0.0 16.5 %copy-start.3 = (s32[4,128]{1,0:T(4,128)S(1)}, s32[4,128]{1,0:T(4,128)}, u32[]{:S(2)}) copy-start(s32[4,128]{1,0:T(4,128)} %stack_ref.1) | copy-start | bytes 6148

commit v5 on v4

--- a/solution.py
+++ b/solution.py
@@ -36,7 +36,7 @@
     return max(k for k in range(1, limit + 1) if stack % k == 0)
 
 
-def gather_plan(gath, sends, receives):
+def gather_plan(gath, used, sends, receives):
     rows, cols = lax.axis_size("row"), lax.axis_size("col")
     plane = cols // 2
     row, col = lax.axis_index("row"), lax.axis_index("col")
@@ -44,23 +44,29 @@
     other = (row, chip * 2 + 1 - core)
     steps = [(a, b) for a in range(rows) for b in range(plane) if a or b]
     steps.sort(key=lambda step: step[0] + step[1].bit_count())
-
-    def place(step):
-        return (mate(row, step[0], rows), mate(chip, step[1], plane) * 2 + core)
+    ranked = [sorted(range(rows), key=lambda other: abs(other - here)) for here in range(rows)]
+
+    def near_row(step):
+        index = ranked[0][step]
+        for here in range(1, rows):
+            index = jnp.where(row == here, ranked[here][step], index)
+        return index
+
+    order = [near_row(step) for step in range(rows)]
+
+    def place(step, twin=False):
+        side = 1 - core if twin else core
+        return (order[step[0]], mate(chip, step[1], plane) * 2 + side)
 
     def slot(step, twin):
-        return (
-            mate(row, step[0], rows) * cols
-            + mate(chip, step[1], plane) * 2
-            + (1 - core if twin else core)
-        )
+        return order[step[0]] * cols + mate(chip, step[1], plane) * 2 + (1 - core if twin else core)
 
     started = []
 
     def send(number, to):
         copy = pltpu.make_async_remote_copy(
-            src_ref=gath.at[number],
-            dst_ref=gath.at[number],
+            src_ref=gath.at[number, 0:used],
+            dst_ref=gath.at[number, 0:used],
             send_sem=sends.at[len(started)],
             recv_sem=receives.at[number],
             device_id=to,
@@ -71,8 +77,8 @@
 
     def arrive(number):
         pltpu.make_async_remote_copy(
-            src_ref=gath.at[number],
-            dst_ref=gath.at[number],
+            src_ref=gath.at[number, 0:used],
+            dst_ref=gath.at[number, 0:used],
             send_sem=sends.at[0],
             recv_sem=receives.at[number],
             device_id=other,
@@ -83,38 +89,53 @@
         mine = slot((0, 0), False)
         for step in reversed(steps):
             send(mine, place(step))
+            if not step[0]:
+                send(mine, place(step, True))
         send(mine, other)
 
-    def finish():
+    def relay():
         for step in steps:
             number = slot(step, False)
             arrive(number)
-            send(number, other)
-        for step in [(0, 0)] + steps:
-            arrive(slot(step, True))
+            if step[0]:
+                send(number, other)
+
+    def collect(row_step):
+        for step in range(plane):
+            arrive(slot((row_step, step), True))
+        return order[row_step]
 
     def drain():
         for copy in started:
             copy.wait_send()
 
-    return [place(step) for step in steps] + [other], begin, finish, drain
+    twins = [place(step, True) for step in steps if not step[0]]
+    return [place(step) for step in steps] + twins + [other], begin, relay, collect, drain
 
 
 def share_kernel(
+    round_in,
+    ocean_in,
+    order_in,
+    order_row,
+    cell_in,
+    stack_in,
+    x_hbm,
+    flat_ref,
+    rounds_s,
     round_s,
     ocean_s,
     order_s,
     order_ref,
     cell_ref,
     stack_ref,
-    x_hbm,
-    flat_ref,
-    rounds_s,
     xt,
     list_v,
     list_s,
     gath,
     one_hot,
+    total_ref,
+    sem_small,
     sem_in,
     sem_list,
     sends,
@@ -126,6 +147,7 @@
     cap = one_hot.shape[0] // devices
     groups = columns // lanes
     parts = lanes // cap
+    used = -(-(members + 1) // parts)
     me = device_number()
     state = [
         pltpu.make_async_copy(
@@ -135,12 +157,26 @@
         )
         for g in range(groups)
     ]
-    for copy in state:
+    pairs = (
+        (order_in, order_s),
+        (cell_in, cell_ref),
+        (stack_in, stack_ref),
+        (round_in, round_s),
+        (order_row, order_ref),
+        (ocean_in, ocean_s),
+    )
+    small = [
+        pltpu.make_async_copy(source, target, sem_small.at[k])
+        for k, (source, target) in enumerate(pairs)
+    ]
+    for copy in small + state:
         copy.start()
-    peers, begin, finish, drain = gather_plan(gath, sends, receives)
+    peers, begin, relay, collect, drain = gather_plan(gath, used, sends, receives)
     barrier = pltpu.get_barrier_semaphore()
     for place in peers:
         pl.semaphore_signal(barrier, inc=1, device_id=place, device_id_type=MESH)
+    for copy in small:
+        copy.wait()
 
     local = cell_ref[...] - order_s[me] * columns
     here = jnp.logical_and(local >= 0, local < columns)
@@ -224,14 +260,14 @@
         cap,
         pick,
         (jnp.zeros((members, lanes), jnp.float32), jnp.zeros((8, lanes), jnp.float32)),
-        unroll=8,
-    )
-    rest = jnp.zeros((parts * piece - members - 8, lanes), jnp.float32)
+        unroll=cap,
+    )
+    rest = jnp.zeros((parts * piece - members, lanes), jnp.float32)
     held = jnp.concatenate([held, flags, rest], axis=0)
     part_of = lax.broadcasted_iota(jnp.int32, (piece, lanes), 1) // cap
     packed = held[0:piece]
     for g in range(1, parts):
-        moved = pltpu.roll(held[g * piece : (g + 1) * piece], g * cap, axis=1)
+        moved = pltpu.roll(held[g * used : g * used + piece], g * cap, axis=1)
         packed = jnp.where(part_of == g, moved, packed)
     gath[me] = packed
 
@@ -240,28 +276,43 @@
     at = lax.broadcasted_iota(jnp.int32, (devices * cap, obs), 0).astype(jnp.float32)
     for b in range(batches):
         one_hot[:, b * obs : (b + 1) * obs] = (slots[b] == at).astype(jnp.bfloat16)
-    finish()
-
-    unpacked = []
-    for g in range(parts):
-        tiles = []
-        for first_device in range(0, devices, parts):
-            tile = None
-            for q in range(parts):
-                moved = gath[first_device + q]
-                if q != g:
-                    moved = pltpu.roll(moved, (q - g) % parts * cap, axis=1)
-                tile = moved if q == 0 else jnp.where(part_of == q, moved, tile)
-            tiles.append(tile)
-        unpacked.append(jnp.concatenate(tiles, axis=1))
-    high, low = split(jnp.concatenate(unpacked, axis=0))
-    placed = jnp.dot(
-        jnp.concatenate([high, low], axis=0), one_hot[...], preferred_element_type=jnp.float32
-    )
-    height = parts * piece
-    placed = placed[0:height] + placed[height:]
-    for b in range(batches):
-        flat_ref[b] = placed[:, b * obs : (b + 1) * obs]
+    relay()
+
+    rows = lax.axis_size("row")
+    share = devices // rows
+    for row_step in range(rows):
+        row = collect(row_step)
+        unpacked = []
+        for g in range(parts):
+            tiles = []
+            for begin_at in range(0, share, parts):
+                tile = None
+                for q in range(parts):
+                    moved = gath[row * share + begin_at + q]
+                    if q != g:
+                        moved = pltpu.roll(moved, (q - g) % parts * cap, axis=1)
+                    tile = moved if q == 0 else jnp.where(part_of == q, moved, tile)
+                tiles.append(tile)
+            unpacked.append(jnp.concatenate(tiles, axis=1))
+        high, low = split(jnp.concatenate(unpacked, axis=0))
+        start = pl.multiple_of(row * (share * cap), share * cap)
+        placed = jnp.dot(
+            jnp.concatenate([high, low], axis=0),
+            one_hot[pl.ds(start, share * cap), :],
+            preferred_element_type=jnp.float32,
+        )
+        placed = placed[0 : parts * piece] + placed[parts * piece :]
+        if row_step == 0:
+            total_ref[...] = placed
+        elif row_step < rows - 1:
+            total_ref[...] += placed
+        else:
+            placed = total_ref[...] + placed
+            placed = jnp.concatenate(
+                [placed[g * piece : g * piece + used] for g in range(parts)], axis=0
+            )
+            for b in range(batches):
+                flat_ref[b, 0 : parts * used] = placed[:, b * obs : (b + 1) * obs]
     drain()
 
 
@@ -491,7 +542,7 @@
     while cap < min(mean + 4 * math.isqrt(mean), 128):
         cap *= 2
     parts = 128 // cap
-    piece = round_up(-(-(members + 8) // parts), 8)
+    piece = round_up(-(-(members + 1) // parts), 8)
     smem = pl.BlockSpec(memory_space=pltpu.SMEM)
     vmem = pl.BlockSpec(memory_space=pltpu.VMEM)
     hbm = pl.BlockSpec(memory_space=pl.ANY)
@@ -505,14 +556,22 @@
                 jax.ShapeDtypeStruct((batches, parts * piece, obs), jnp.float32),
                 jax.ShapeDtypeStruct((1,), jnp.int32),
             ),
-            in_specs=[smem, smem, smem, vmem, vmem, vmem, hbm],
+            in_specs=[hbm] * 7,
             out_specs=(vmem, smem),
             scratch_shapes=[
+                pltpu.SMEM((1,), jnp.int32),
+                pltpu.SMEM((columns,), jnp.int32),
+                pltpu.SMEM((devices,), jnp.int32),
+                pltpu.VMEM((1, devices), jnp.int32),
+                pltpu.VMEM((batches, obs), jnp.int32),
+                pltpu.VMEM((batches, obs), jnp.int32),
                 pltpu.VMEM((columns // 128 * stack, members, 128), jnp.float32),
                 pltpu.VMEM((1, obs), jnp.int32),
                 pltpu.SMEM((1, obs), jnp.int32),
                 pltpu.VMEM((devices, piece, 128), jnp.float32),
                 pltpu.VMEM((devices * cap, batches * obs), jnp.bfloat16),
+                pltpu.VMEM((parts * piece, batches * obs), jnp.float32),
+                pltpu.SemaphoreType.DMA((6,)),
                 pltpu.SemaphoreType.DMA((columns // 128,)),
                 pltpu.SemaphoreType.DMA,
                 pltpu.SemaphoreType.DMA((devices,)),

time: 29 us -> 27.7 us (0.955)
  Pallas kernels: 28.1 us -> 26.7 us
    pallas_call x1, Pallas kernels: 16.5 us -> 15.1 us  [share(): pl.pallas_call(share_kernel, out_shape=(jax.ShapeDtypeStruct((batches, pa...]
where the time goes in v5:
time: 27.7 us; the launch traced here: 27.6 us
  Pallas kernels  26.7 us (96%)
  loops' own time  0.69 us (2%)
    pallas_call x1, Pallas kernels, share(): pl.pallas_call(share_kernel, out_shape=(jax.ShapeDtypeStruct((batches, pa...  15.1 us
    pallas_call x1, Pallas kernels, per_device(): pl.pallas_call(update_kernel, out_shape=jax.ShapeDtypeStruct(levels.shape...  11.6 us
    another operation x1, loops' own time, per_device(): lax.while_loop(lambda carry: carry[0] < rounds[0], lambda carry: (carry[0...  0.69 us

profile of v5, /device:TPU:1, one launch (start us, length us, event | category | flops | bytes accessed | tf_op | source)
XLA Modules:
  0.0 27.6 jit_solution(4310390725864538000)
XLA Ops:
  0.0 0.0 copy-start.2
  0.0 0.0 copy-start.1
  0.0 0.0 copy-start
  0.0 0.0 copy-start.3
  0.0 15.1 %share.2 = (f32[4,96,128]{2,1,0:T(8,128)S(1)}, s32[1]{0:T(128)}) custom-call(s32[1]{0:T(128)} %constant.2.clone.1.round_in, s32[512]{0:T(512)} %ocean_in.1, s32[32]{0:T(128)} %order_s.1, s32[1,32]{1,0:T(1,128)} %bitcast.15, s32[4,128]{1,0:T(4,128)} %cell_ref.1, s32[4,128]{1,0:T(4,128)} %stack_in.1, f32[30,80,512]{2,1,0:T(8,128)} %bitcast.12), custom_call_target="tpu_custom_call" | custom-call | tf_op jit(solution)/shard_map/share/pallas_call | solution.py:553
  15.1 0.0 copy-done.2
  15.1 0.0 copy-done.1
  15.1 0.0 copy-done
  15.1 0.0 copy-done.3
  15.1 0.7 %while.10 = (s32[]{:T(128)}, f32[4,96,128]{2,1,0:T(8,128)S(1)}, s32[1]{0:T(128)}, s32[32]{0:T(128)S(1)}, s32[512]{0:T(512)S(1)}, /*index=5*/s32[4,128]{1,0:T(4,1...) while((s32[]{:T(128)}, f32[4,96,128]{2,1,0:T(8,128)S(1)}, s32[1]{0:T(128)}, s32[32]{0:T(128)S(1)}, ...), condition=%wide.region_1.0_spmd, body=%wide.region_0.0_spmd.sunk | while | flops 49154 | bytes 589925 | solution.py:585
  15.8 11.6 %update.1 = f32[30,80,512]{2,1,0:T(8,128)} custom-call(s32[32]{0:T(128)S(1)} %get-tuple-element.152, s32[1,512]{1,0:T(1,128)S(1)} %bitcast.14, s32[4,128]{1,0:T(4,128)S(1)} %get-tuple-element.151, s32[4,128]{1,0:T(4,128)} %start_ref.1, s32[4,128]{1,0:T(4,128)} %span_ref.1, f32[4,128]{1,0:T(4,128)} %value_ref.1, f32[4,128,128]{2,1,0:T(8,128)} %mean_ref.1, ...), custom_call_target="tpu_custom_call" | custom-call | tf_op jit(solution)/shard_map/update/pallas_call | solution.py:591
Async XLA Ops:
  0.0 15.1 %copy-start.2 = (s32[32]{0:T(128)S(1)}, s32[32]{0:T(128)}, u32[]{:S(2)}) copy-start(s32[32]{0:T(128)} %order_s.1) | copy-start | bytes 388
  0.0 15.1 %copy-start.1 = (s32[4,128]{1,0:T(4,128)S(1)}, s32[4,128]{1,0:T(4,128)}, u32[]{:S(2)}) copy-start(s32[4,128]{1,0:T(4,128)} %cell_ref.1) | copy-start | bytes 6148
  0.0 15.1 %copy-start = (s32[512]{0:T(512)S(1)}, s32[512]{0:T(512)}, u32[]{:S(2)}) copy-start(s32[512]{0:T(512)} %ocean_in.1) | copy-start | bytes 6148
  0.0 15.1 %copy-start.3 = (s32[4,128]{1,0:T(4,128)S(1)}, s32[4,128]{1,0:T(4,128)}, u32[]{:S(2)}) copy-start(s32[4,128]{1,0:T(4,128)} %stack_in.1) | copy-start | bytes 6148

commit v6 on v5

--- a/solution.py
+++ b/solution.py
@@ -11,6 +11,7 @@
 MESH = pl.DeviceIdType.MESH
 NT = (((1,), (1,)), ((), ()))
 SIZES = (48, 80)
+SHARE_REFS = 20
 
 
 def device_number():
@@ -121,6 +122,21 @@
     cell_in,
     stack_in,
     x_hbm,
+    *rest,
+):
+    extra = (len(rest) - SHARE_REFS) // 2
+    ahead_in, rest = rest[:extra], rest[extra:]
+    ahead_out, rest = rest[2 : 2 + extra], rest[:2] + rest[2 + extra :]
+    share_body(
+        (round_in, ocean_in, order_in, order_row, cell_in, stack_in, x_hbm),
+        tuple(zip(ahead_in, ahead_out)),
+        *rest,
+    )
+
+
+def share_body(
+    inputs,
+    handed,
     flat_ref,
     rounds_s,
     round_s,
@@ -135,12 +151,14 @@
     gath,
     one_hot,
     total_ref,
+    sem_handed,
     sem_small,
     sem_in,
     sem_list,
     sends,
     receives,
 ):
+    round_in, ocean_in, order_in, order_row, cell_in, stack_in, x_hbm = inputs
     stack, members, columns = x_hbm.shape
     batches, obs = cell_ref.shape
     devices, piece, lanes = gath.shape
@@ -273,6 +291,12 @@
 
     pl.semaphore_wait(barrier, len(peers))
     begin()
+    handed = [
+        pltpu.make_async_copy(source, target, sem_handed.at[k])
+        for k, (source, target) in enumerate(handed)
+    ]
+    for copy in handed:
+        copy.start()
     at = lax.broadcasted_iota(jnp.int32, (devices * cap, obs), 0).astype(jnp.float32)
     for b in range(batches):
         one_hot[:, b * obs : (b + 1) * obs] = (slots[b] == at).astype(jnp.bfloat16)
@@ -313,6 +337,8 @@
             )
             for b in range(batches):
                 flat_ref[b, 0 : parts * used] = placed[:, b * obs : (b + 1) * obs]
+    for copy in handed:
+        copy.wait()
     drain()
 
 
@@ -549,15 +575,18 @@
 
     levels = jnp.transpose(prior, (1, 0, 2))
 
+    ahead = (window_start, window_span, obs_values, gain_mean, gain_spread)
+
     def share(number):
         return pl.pallas_call(
             share_kernel,
             out_shape=(
                 jax.ShapeDtypeStruct((batches, parts * piece, obs), jnp.float32),
                 jax.ShapeDtypeStruct((1,), jnp.int32),
-            ),
-            in_specs=[hbm] * 7,
-            out_specs=(vmem, smem),
+            )
+            + tuple(jax.ShapeDtypeStruct(array.shape, array.dtype) for array in ahead),
+            in_specs=[hbm] * (7 + len(ahead)),
+            out_specs=(vmem, smem) + (vmem,) * len(ahead),
             scratch_shapes=[
                 pltpu.SMEM((1,), jnp.int32),
                 pltpu.SMEM((columns,), jnp.int32),
@@ -571,17 +600,20 @@
                 pltpu.VMEM((devices, piece, 128), jnp.float32),
                 pltpu.VMEM((devices * cap, batches * obs), jnp.bfloat16),
                 pltpu.VMEM((parts * piece, batches * obs), jnp.float32),
+                pltpu.SemaphoreType.DMA((max(len(ahead), 1),)),
                 pltpu.SemaphoreType.DMA((6,)),
                 pltpu.SemaphoreType.DMA((columns // 128,)),
                 pltpu.SemaphoreType.DMA,
                 pltpu.SemaphoreType.DMA((devices,)),
                 pltpu.SemaphoreType.DMA((devices,)),
             ],
-            compiler_params=pltpu.CompilerParams(collective_id=0, has_side_effects=True),
+            compiler_params=pltpu.CompilerParams(
+                collective_id=0, has_side_effects=True, vmem_limit_bytes=24 * 2**20
+            ),
             name="share",
-        )(number, ocean_mask, tile_order, tile_order.reshape(1, devices), obs_cell, obs_stack, levels)
-
-    shared, rounds = share(jnp.zeros((1,), jnp.int32))
+        )(number, ocean_mask, tile_order, tile_order.reshape(1, devices), obs_cell, obs_stack, levels, *ahead)
+
+    shared, rounds, *handed = share(jnp.zeros((1,), jnp.int32))
     _, shared = lax.while_loop(
         lambda carry: carry[0] < rounds[0],
         lambda carry: (carry[0] + 1, carry[1] + share(carry[0].reshape(1))[0]),
@@ -604,16 +636,13 @@
             pltpu.SemaphoreType.DMA((stack,)),
             pltpu.SemaphoreType.DMA((stack,)),
         ],
+        compiler_params=pltpu.CompilerParams(vmem_limit_bytes=32 * 2**20),
         name="update",
     )(
         tile_order,
         ocean_mask.reshape(1, columns),
         obs_cell,
-        window_start,
-        window_span,
-        obs_values,
-        gain_mean,
-        gain_spread,
+        *handed,
         shared,
         levels,
     )

time: 27.7 us -> 27.4 us (0.989)
  Pallas kernels: 26.7 us -> 26.3 us
    pallas_call x1, Pallas kernels: 11.6 us -> 11.2 us  [per_device(): pl.pallas_call(update_kernel, out_shape=jax.ShapeDtypeStruct(levels.shape...]
where the time goes in v6:
time: 27.4 us; the launch traced here: 27.2 us
  Pallas kernels  26.3 us (96%)
  loops' own time  0.55 us (2%)
  between operations  0.3 us (1%)
    pallas_call x1, Pallas kernels, share(): pl.pallas_call(share_kernel, out_shape=(jax.ShapeDtypeStruct((batches, pa...  15.1 us
    pallas_call x1, Pallas kernels, per_device(): pl.pallas_call(update_kernel, out_shape=jax.ShapeDtypeStruct(levels.shape...  11.2 us
    another operation x1, loops' own time, per_device(): lax.while_loop(lambda carry: carry[0] < rounds[0], lambda carry: (carry[0...  0.55 us

profile of v6, /device:TPU:1, one launch (start us, length us, event | category | flops | bytes accessed | tf_op | source)
XLA Modules:
  0.0 27.2 jit_solution(16161715384530942542)
XLA Ops:
  0.0 0.0 copy-start.4
  0.0 0.0 copy-start.3
  0.0 0.0 copy-start.2
  0.0 0.0 copy-start.1
  0.0 0.0 copy-start
  0.0 0.0 copy-start.7
  0.0 0.0 copy-start.6
  0.0 0.0 copy-start.8
  0.1 0.0 copy-start.5
  0.1 15.1 %share.2 = (f32[4,96,128]{2,1,0:T(8,128)S(1)}, s32[1]{0:T(128)}, s32[4,128]{1,0:T(4,128)S(1)}, s32[4,128]{1,0:T(4,128)S(1)}, f32[4,128]{1,0:T(4,128)S(1)}, /*ind...) custom-call(s32[1]{0:T(128)} %constant.1.clone.1.round_in, s32[512]{0:T(512)} %ocean_in.1, s32[32]{0:T(128)} %order_s.1, ...), custom_call_target="tpu_custom_call" | custom-call | tf_op jit(solution)/shard_map/share/pallas_call | solution.py:581
  15.2 0.0 copy-done.4
  15.2 0.0 copy-done.3
  15.2 0.0 copy-done.2
  15.2 0.0 copy-done.1
  15.2 0.0 copy-done
  15.3 0.0 copy-done.7
  15.3 0.0 copy-done.6
  15.3 0.0 copy-done.8
  15.3 0.0 copy-done.5
  15.3 0.6 %while.10 = (s32[]{:T(128)}, f32[4,96,128]{2,1,0:T(8,128)S(1)}, s32[1]{0:T(128)}, s32[32]{0:T(128)S(1)}, s32[512]{0:T(512)S(1)}, /*index=5*/s32[4,128]{1,0:T(4,1...) while((s32[]{:T(128)}, f32[4,96,128]{2,1,0:T(8,128)S(1)}, ...), condition=%wide.region_1.0_spmd, body=%wide.region_0.0_spmd.sunk | while | flops 49154 | bytes 589965 | solution.py:617
  15.9 11.2 %update.1 = f32[30,80,512]{2,1,0:T(8,128)} custom-call(s32[32]{0:T(128)S(1)} %get-tuple-element.242, s32[1,512]{1,0:T(1,128)S(1)} %bitcast.14, s32[4,128]{1,0:T(4,128)S(1)} %get-tuple-element.241, s32[4,128]{1,0:T(4,128)S(1)} %get-tuple-element.81.start_ref, s32[4,128]{1,0:T(4,128)S(1)} %get-tuple-element.82.span_ref, ...), custom_call_target="tpu_custom_call" | custom-call | tf_op jit(solution)/shard_map/update/pallas_call | solution.py:623
Async XLA Ops:
  0.0 15.2 %copy-start.4 = (s32[32]{0:T(128)S(1)}, s32[32]{0:T(128)}, u32[]{:S(2)}) copy-start(s32[32]{0:T(128)} %order_s.1) | copy-start | bytes 388
  0.0 15.2 %copy-start.3 = (s32[4,128]{1,0:T(4,128)S(1)}, s32[4,128]{1,0:T(4,128)}, u32[]{:S(2)}) copy-start(s32[4,128]{1,0:T(4,128)} %cell_ref.1) | copy-start | bytes 6148
  0.0 15.2 %copy-start.2 = (s32[512]{0:T(512)S(1)}, s32[512]{0:T(512)}, u32[]{:S(2)}) copy-start(s32[512]{0:T(512)} %ocean_in.1) | copy-start | bytes 6148
  0.0 15.2 %copy-start.1 = (f32[4,128,128]{2,1,0:T(8,128)S(1)}, f32[4,128,128]{2,1,0:T(8,128)}, u32[]{:S(2)}) copy-start(f32[4,128,128]{2,1,0:T(8,128)} %rest_4_.1) | copy-start | bytes 786436
  0.0 15.2 %copy-start = (f32[4,128,128]{2,1,0:T(8,128)S(1)}, f32[4,128,128]{2,1,0:T(8,128)}, u32[]{:S(2)}) copy-start(f32[4,128,128]{2,1,0:T(8,128)} %rest_3_.1) | copy-start | bytes 786436
  0.0 15.2 %copy-start.7 = (s32[4,128]{1,0:T(4,128)S(1)}, s32[4,128]{1,0:T(4,128)}, u32[]{:S(2)}) copy-start(s32[4,128]{1,0:T(4,128)} %rest_1_.1) | copy-start | bytes 6148
  0.0 15.2 %copy-start.6 = (s32[4,128]{1,0:T(4,128)S(1)}, s32[4,128]{1,0:T(4,128)}, u32[]{:S(2)}) copy-start(s32[4,128]{1,0:T(4,128)} %rest_0_.1) | copy-start | bytes 6148
  0.0 15.2 %copy-start.8 = (f32[4,128]{1,0:T(4,128)S(1)}, f32[4,128]{1,0:T(4,128)}, u32[]{:S(2)}) copy-start(f32[4,128]{1,0:T(4,128)} %rest_2_.1) | copy-start | bytes 6148
  0.1 15.2 %copy-start.5 = (s32[4,128]{1,0:T(4,128)S(1)}, s32[4,128]{1,0:T(4,128)}, u32[]{:S(2)}) copy-start(s32[4,128]{1,0:T(4,128)} %stack_in.1) | copy-start | bytes 6148

commit v7 on v6

--- a/solution.py
+++ b/solution.py
@@ -479,6 +479,8 @@
             lows = lax.dot_general(side_d[b, 1], pick, NT, preferred_element_type=jnp.float32)
             parts = jnp.concatenate([highs, highs, lows], axis=1).astype(jnp.bfloat16)
             lhs_d[b, 0:members, 0 : 3 * kept] = parts
+            if kept == obs:
+                continue
             if second:
                 cross = jnp.dot(
                     lhs_a[b // 2, rows],
@@ -495,7 +497,20 @@
             for v in levels:
                 incoming(v).wait()
             values = [xt[v] for v in levels]
-            for b in range(0, batches, 2):
+            for b in range(batches if kept == obs else 0):
+                gains = []
+                for k in range(together):
+                    gain = weight[b] * jnp.dot(
+                        lhs_a[b // 2, b % 2 * obs : b % 2 * obs + obs],
+                        triple(values[k], 0),
+                        preferred_element_type=jnp.float32,
+                    )
+                    gains.append(triple(gain, 0))
+                for k in range(together):
+                    values[k] = values[k] + jnp.dot(
+                        lhs_d[b, 0:members], gains[k], preferred_element_type=jnp.float32
+                    )
+            for b in range(0, batches if kept < obs else 0, 2):
                 both = []
                 for k in range(together):
                     both.append(

time: 27.4 us -> 27.2 us (level)
  no operation moved by 1% of the time
where the time goes in v7:
time: 27.2 us; the launch traced here: 27.1 us
  Pallas kernels  26.3 us (97%)
  loops' own time  0.55 us (2%)
    pallas_call x1, Pallas kernels, share(): pl.pallas_call(share_kernel, out_shape=(jax.ShapeDtypeStruct((batches, pa...  15.1 us
    pallas_call x1, Pallas kernels, per_device(): pl.pallas_call(update_kernel, out_shape=jax.ShapeDtypeStruct(levels.shape...  11.2 us
    another operation x1, loops' own time, per_device(): lax.while_loop(lambda carry: carry[0] < rounds[0], lambda carry: (carry[0...  0.55 us

profile of v7, /device:TPU:1, one launch (start us, length us, event | category | flops | bytes accessed | tf_op | source)
XLA Modules:
  0.0 27.1 jit_solution(18374948715683976738)
XLA Ops:
  0.0 0.0 copy-start.4
  0.0 0.0 copy-start.3
  0.0 0.0 copy-start.2
  0.0 0.0 copy-start.1
  0.0 0.0 copy-start
  0.0 0.0 copy-start.7
  0.0 0.0 copy-start.6
  0.0 0.0 copy-start.8
  0.1 0.0 copy-start.5
  0.1 15.1 %share.2 = (f32[4,96,128]{2,1,0:T(8,128)S(1)}, s32[1]{0:T(128)}, s32[4,128]{1,0:T(4,128)S(1)}, s32[4,128]{1,0:T(4,128)S(1)}, f32[4,128]{1,0:T(4,128)S(1)}, /*ind...) custom-call(s32[1]{0:T(128)} %constant.1.clone.1.round_in, s32[512]{0:T(512)} %ocean_in.1, s32[32]{0:T(128)} %order_s.1, ...), custom_call_target="tpu_custom_call" | custom-call | tf_op jit(solution)/shard_map/share/pallas_call | solution.py:596
  15.2 0.0 copy-done.4
  15.2 0.0 copy-done.3
  15.2 0.0 copy-done.2
  15.2 0.0 copy-done.1
  15.2 0.0 copy-done
  15.3 0.0 copy-done.7
  15.3 0.0 copy-done.6
  15.3 0.0 copy-done.8
  15.3 0.0 copy-done.5
  15.3 0.6 %while.10 = (s32[]{:T(128)}, f32[4,96,128]{2,1,0:T(8,128)S(1)}, s32[1]{0:T(128)}, s32[32]{0:T(128)S(1)}, s32[512]{0:T(512)S(1)}, /*index=5*/s32[4,128]{1,0:T(4,1...) while((s32[]{:T(128)}, f32[4,96,128]{2,1,0:T(8,128)S(1)}, ...), condition=%wide.region_1.0_spmd, body=%wide.region_0.0_spmd.sunk | while | flops 49154 | bytes 589965 | solution.py:632
  15.9 11.2 %update.1 = f32[30,80,512]{2,1,0:T(8,128)} custom-call(s32[32]{0:T(128)S(1)} %get-tuple-element.242, s32[1,512]{1,0:T(1,128)S(1)} %bitcast.14, s32[4,128]{1,0:T(4,128)S(1)} %get-tuple-element.241, s32[4,128]{1,0:T(4,128)S(1)} %get-tuple-element.81.start_ref, s32[4,128]{1,0:T(4,128)S(1)} %get-tuple-element.82.span_ref, ...), custom_call_target="tpu_custom_call" | custom-call | tf_op jit(solution)/shard_map/update/pallas_call | solution.py:638
Async XLA Ops:
  0.0 15.2 %copy-start.4 = (s32[32]{0:T(128)S(1)}, s32[32]{0:T(128)}, u32[]{:S(2)}) copy-start(s32[32]{0:T(128)} %order_s.1) | copy-start | bytes 388
  0.0 15.2 %copy-start.3 = (s32[4,128]{1,0:T(4,128)S(1)}, s32[4,128]{1,0:T(4,128)}, u32[]{:S(2)}) copy-start(s32[4,128]{1,0:T(4,128)} %cell_ref.1) | copy-start | bytes 6148
  0.0 15.2 %copy-start.2 = (s32[512]{0:T(512)S(1)}, s32[512]{0:T(512)}, u32[]{:S(2)}) copy-start(s32[512]{0:T(512)} %ocean_in.1) | copy-start | bytes 6148
  0.0 15.2 %copy-start.1 = (f32[4,128,128]{2,1,0:T(8,128)S(1)}, f32[4,128,128]{2,1,0:T(8,128)}, u32[]{:S(2)}) copy-start(f32[4,128,128]{2,1,0:T(8,128)} %rest_4_.1) | copy-start | bytes 786436
  0.0 15.2 %copy-start = (f32[4,128,128]{2,1,0:T(8,128)S(1)}, f32[4,128,128]{2,1,0:T(8,128)}, u32[]{:S(2)}) copy-start(f32[4,128,128]{2,1,0:T(8,128)} %rest_3_.1) | copy-start | bytes 786436
  0.0 15.2 %copy-start.7 = (s32[4,128]{1,0:T(4,128)S(1)}, s32[4,128]{1,0:T(4,128)}, u32[]{:S(2)}) copy-start(s32[4,128]{1,0:T(4,128)} %rest_1_.1) | copy-start | bytes 6148
  0.0 15.2 %copy-start.6 = (s32[4,128]{1,0:T(4,128)S(1)}, s32[4,128]{1,0:T(4,128)}, u32[]{:S(2)}) copy-start(s32[4,128]{1,0:T(4,128)} %rest_0_.1) | copy-start | bytes 6148
  0.0 15.2 %copy-start.8 = (f32[4,128]{1,0:T(4,128)S(1)}, f32[4,128]{1,0:T(4,128)}, u32[]{:S(2)}) copy-start(f32[4,128]{1,0:T(4,128)} %rest_2_.1) | copy-start | bytes 6148
  0.1 15.2 %copy-start.5 = (s32[4,128]{1,0:T(4,128)S(1)}, s32[4,128]{1,0:T(4,128)}, u32[]{:S(2)}) copy-start(s32[4,128]{1,0:T(4,128)} %stack_in.1) | copy-start | bytes 6148
